TPU v7x, 32 devices: a whole 2x2x4 slice. The times are simulated.
32 devices in a mesh: rows: 8 (over z, x), grp: 4 (over y, core).
Axes of the slice: x: 2, y: 2, z: 4, core: 2. Of those that a mesh axis runs over, the one named last changes fastest.
Arguments:
- matrix: bfloat16 [10240, 16384], P(('rows', 'grp')), may hold values from -36 to 36
- sample_rows: int32 [32, 128, 256], P(('rows', 'grp')), may hold values from 0 to 319
- pair_list: int32 [8, 8, 4], replicated, may hold values from 0 to 255, as said below
- pair_count: int32 [8, 8], replicated, may hold values from 1 to 4, as said below
- pair_blocks: int32 [256, 2], replicated, may hold values from 0 to 127, as said below
Outputs:
- gram: float32 [256, 128, 128], P(('rows', 'grp'))
Inputs may be any that keep to these rules, and one draw needn't show every extreme that they name: `pair_list`: entry [s, r, k] lies in [r * 32, (r + 1) * 32); the 4 entries of one [s, r] are distinct. `pair_count`: every row group has some owner with all 4 slots active, and some owner has all 4 slots active from every row group. `pair_blocks`: the two blocks of a pair differ.
All inputs are finite; a program needn't handle non-finite values.
Results may differ from a plain program's by a relative error of at most 0.0016.
Values sent between devices are 32-bit elements; how exact they have to be, the bound alone decides.
No kernel may reach another device: no remote copies, remote signals or barrier semaphores. Data moves between devices by JAX's collectives and lax.ppermute only.
A program may use at most 192 MiB of HBM per device.

v0:
```python
import functools

import jax
import jax.numpy as jnp
from jax import lax
from jax.experimental import pallas as pl
from jax.experimental.pallas import tpu as pltpu
from jax.sharding import PartitionSpec as P

epsilon = 1e-06
unroll = 4
pieces = 16
late_slots = 1


class Dims:
    def __init__(self, mesh, matrix, sample_rows, pair_list, pair_blocks):
        self.rows_axis = mesh.shape["rows"]
        self.grp_axis = mesh.shape["grp"]
        self.rows_dev, self.columns = matrix.shape
        self.blocks = sample_rows.shape[1]
        self.samples = sample_rows.shape[2]
        self.width = self.columns // self.blocks
        self.cap = pair_list.shape[2]
        self.pairs = pair_blocks.shape[0]
        self.region = self.pairs // self.rows_axis
        self.own = self.region // self.grp_axis
        self.part = self.width // self.grp_axis
        self.rows_total = self.rows_dev * self.rows_axis * self.grp_axis


def list_live(n, first, last, live, counts):
    me = lax.axis_index("rows")

    def scan(o, found):
        r = jnp.bitwise_xor(o, me)
        top = jnp.minimum(counts[me, r], last)

        def add(k, found):
            live[found] = o * n.cap + k
            return found + 1

        return lax.fori_loop(first, top, add, found)

    return lax.fori_loop(0, n.rows_axis, scan, 0)


def multiply(n, first, slots, loads, samples, blocks_of, stage, outs):
    g = lax.axis_index("grp")
    positions = lax.broadcasted_iota(jnp.int32, (n.rows_dev, n.samples), 0)
    ones = jnp.ones((n.samples, n.width), jnp.bfloat16)
    for u, t in enumerate(slots):
        drawn = samples[0, pl.ds(blocks_of(t)[0], 1), :]
        hit = jnp.where(drawn == positions, 1.0, 0.0).astype(jnp.bfloat16)
        times = jnp.dot(hit, ones, preferred_element_type=jnp.float32)
        left, right = loads(u, t)
        weighted = (times * left.astype(jnp.float32)).astype(jnp.bfloat16)
        stage[u] = lax.dot_general(
            weighted, right, (((0,), (0,)), ((), ())), preferred_element_type=jnp.float32
        )
    for u, t in enumerate(slots):
        o = t // n.cap
        row = pl.multiple_of((t % n.cap - first) * n.part, n.part)
        for d in range(n.grp_axis):
            q = pl.multiple_of(jnp.bitwise_xor(g, d) * n.part, n.part)
            outs[d][o, pl.ds(row, n.part), :] = stage[u, pl.ds(q, n.part), :]


def split_outs(n, refs):
    return [refs[0].at[d // 2] if d % 2 else refs[1 + d // 2] for d in range(n.grp_axis)]


def clear(outs, n, rows):
    zero = jnp.zeros((rows, n.width), jnp.float32)

    def body(o, carry):
        for out in outs:
            out[o, pl.ds(0, rows), :] = zero
        return carry

    lax.fori_loop(0, n.rows_axis, body, 0)


def early_kernel(n, last, lists, counts, pairs, samples, matrix, *rest):
    outs = split_outs(n, rest[: 1 + n.grp_axis // 2])
    held, stage, live, arrive = rest[1 + n.grp_axis // 2 :]
    me = lax.axis_index("rows")

    def blocks_of(t):
        pair = lists[me, t % n.cap, jnp.bitwise_xor(t // n.cap, me)]
        return pairs[0, pair], pairs[1, pair]

    def copies(i, t):
        both = blocks_of(t)
        return [
            pltpu.make_async_copy(
                matrix.at[:, pl.ds(pl.multiple_of(both[side] * n.width, n.width), n.width)],
                held.at[i, side],
                arrive.at[i],
            )
            for side in range(2)
        ]

    found = list_live(n, 0, last, live, counts)

    def begin(i, carry):
        for copy in copies(i, live[i]):
            copy.start()
        return carry

    lax.fori_loop(0, found, begin, 0)
    clear(outs, n, last * n.part)

    def group(i, carry):
        at = [jnp.where(i * unroll + u < found, i * unroll + u, 0) for u in range(unroll)]
        slots = [live[a] for a in at]
        for u in range(unroll):

            @pl.when(i * unroll + u < found)
            def _(u=u):
                for copy in copies(at[u], slots[u]):
                    copy.wait()

        def loads(u, t):
            return held[at[u], 0], held[at[u], 1]

        multiply(n, 0, slots, loads, samples, blocks_of, stage, outs)
        return carry

    lax.fori_loop(0, pl.cdiv(found, unroll), group, 0)


def late_kernel(n, first, lists, counts, pairs, samples, matrix, after, *rest):
    outs = split_outs(n, rest[: 1 + n.grp_axis // 2])
    local, sums, stage, live, arrive = rest[1 + n.grp_axis // 2 :]
    me = lax.axis_index("rows")
    g = lax.axis_index("grp")
    piece_blocks = n.blocks // pieces
    piece = piece_blocks * n.width
    tile_rows = (n.cap - first) * n.part

    def copy(i):
        span = pl.ds(i * piece, piece)
        return pltpu.make_async_copy(matrix.at[:, span], local.at[:, span], arrive.at[i])

    for i in range(pieces):
        copy(i).start()
    found = list_live(n, first, n.cap, live, counts)
    clear(outs, n, tile_rows)

    def columns(b):
        return local[:, pl.ds(pl.multiple_of(b * n.width, n.width), n.width)]

    def block_sum(b, carry):
        x = columns(b).astype(jnp.float32)
        sums[pl.ds(b, 1), :] = jnp.sum(x * x, axis=0, keepdims=True)
        return carry

    for i in range(pieces):
        copy(i).wait()
        lax.fori_loop(i * piece_blocks, (i + 1) * piece_blocks, block_sum, 0, unroll=2)

    for d in range(n.grp_axis):

        def place(o, carry, d=d):
            base = (jnp.bitwise_xor(o, me) * n.grp_axis + jnp.bitwise_xor(g, d)) * n.own
            for j in range(n.own):
                for side in range(2):
                    b = pairs[side, base + j]
                    outs[d][o, pl.ds(tile_rows + 2 * j + side, 1), :] = sums[pl.ds(b, 1), :]
            return carry

        lax.fori_loop(0, n.rows_axis, place, 0)

    def blocks_of(t):
        pair = lists[me, t % n.cap, jnp.bitwise_xor(t // n.cap, me)]
        return pairs[0, pair], pairs[1, pair]

    def group(i, carry):
        slots = [live[jnp.where(i * unroll + u < found, i * unroll + u, 0)] for u in range(unroll)]

        def loads(u, t):
            both = blocks_of(t)
            return columns(both[0]), columns(both[1])

        multiply(n, first, slots, loads, samples, blocks_of, stage, outs)
        return carry

    lax.fori_loop(0, pl.cdiv(found, unroll), group, 0)


def spread_kernel(n, *refs):
    halves = [refs[:3], refs[3:6]]
    outs = refs[6:]
    for o in range(n.rows_axis):
        at = 0
        for kept, core, chip in halves:
            rows = kept.shape[1]
            outs[o][pl.ds(at, rows), :] = kept[o] + core[0, o] + chip[o]
            at += rows


def gather_kernel(n, lists, *refs):
    parts = refs[: n.rows_axis]
    outs = refs[n.rows_axis : n.rows_axis + n.grp_axis]
    total, acc = refs[n.rows_axis + n.grp_axis :]
    me = lax.axis_index("rows")
    g = lax.axis_index("grp")
    acc[...] = jnp.zeros_like(acc)
    column = jnp.zeros((2 * n.own, n.width), jnp.float32)
    for o in range(n.rows_axis):
        source = jnp.bitwise_xor(me, o)
        for k in range(n.cap):
            i = lists[source, k, me] - me * n.region
            acc[i] += parts[o][pl.ds(k * n.part, n.part), :]
        column = column + parts[o][pl.ds(n.cap * n.part, 2 * n.own), :]
    total[...] = column
    for d in range(n.grp_axis):
        outs[d][...] = acc[pl.ds(jnp.bitwise_xor(g, d) * n.own, n.own)]


def factor_kernel(n, total, out):
    root = jnp.sqrt(total[...] / n.rows_total + epsilon)
    for j in range(n.own):
        left = jnp.transpose(jnp.broadcast_to(root[2 * j : 2 * j + 1], (n.width, n.width)))
        out[j] = 1.0 / (n.samples * left * root[2 * j + 1 : 2 * j + 2])


def scale_kernel(n, factor, *refs):
    parts = refs[: n.grp_axis]
    out = refs[n.grp_axis]
    g = lax.axis_index("grp")
    for d in range(n.grp_axis):
        q = pl.ds(pl.multiple_of(jnp.bitwise_xor(g, d) * n.part, n.part), n.part)
        for j in range(n.own):
            out[j, q, :] = parts[d][j] * factor[j, q, :]


def swap(x, axis, size, distance):
    return lax.ppermute(x, axis, [(i, i ^ distance) for i in range(size)])


def megabytes(*shapes):
    total = sum(4 * functools.reduce(lambda a, b: a * b, s) for s in shapes)
    return pltpu.CompilerParams(vmem_limit_bytes=int(total) + (2 << 20))


def shards(mesh, matrix, sample_rows, pair_list, pair_count, pair_blocks):
    n = Dims(mesh, matrix, sample_rows, pair_list, pair_blocks)
    f32 = jnp.float32
    vmem = pl.BlockSpec(memory_space=pltpu.VMEM)
    smem = pl.BlockSpec(memory_space=pltpu.SMEM)
    hbm = pl.BlockSpec(memory_space=pl.ANY)
    matrix = pltpu.with_memory_space_constraint(matrix, pltpu.HBM)
    lists = jnp.transpose(pair_list, (0, 2, 1))
    pairs = jnp.transpose(pair_blocks)
    half = n.grp_axis // 2
    first = n.cap - late_slots

    def stage_outs(rows):
        one = (n.rows_axis, rows, n.width)
        return [jax.ShapeDtypeStruct((half,) + one, f32)] + [jax.ShapeDtypeStruct(one, f32)] * half

    stage = (unroll, n.width, n.width)
    slots = n.rows_axis * first
    rows = first * n.part
    early = pl.pallas_call(
        functools.partial(early_kernel, n, first),
        out_shape=stage_outs(rows),
        in_specs=[smem, smem, smem, vmem, hbm],
        out_specs=[vmem] * (1 + half),
        scratch_shapes=[
            pltpu.VMEM((slots, 2, n.rows_dev, n.width), matrix.dtype),
            pltpu.VMEM(stage, f32),
            pltpu.SMEM((slots,), jnp.int32),
            pltpu.SemaphoreType.DMA((slots,)),
        ],
        compiler_params=megabytes(
            (slots, n.rows_dev, n.width), stage, sample_rows.shape, (n.grp_axis, n.rows_axis, rows, n.width)
        ),
        name="early_tiles",
    )(lists, pair_count, pairs, sample_rows, matrix)

    def reduce_scatter(outs):
        got = swap(outs[0], "grp", n.grp_axis, 1)
        kept = {2 * i: outs[1 + i] + got[i] for i in range(1, half)}
        sent = kept[half]
        result = [outs[1], got]
        distance = 2
        while distance < n.grp_axis:
            came = {d: swap(kept[d], "grp", n.grp_axis, distance) for d in kept if d & distance}
            result.append(came.pop(distance))
            kept = {d: kept[d] + came[d + distance] for d in kept if not d & distance}
            distance *= 2
        chips = result[2]
        for more in result[3:]:
            chips = chips + more
        return [outs[1], got, chips], sent

    early_sums, sent = reduce_scatter(early)
    late_rows = late_slots * n.part + 2 * n.own
    slots = n.rows_axis * late_slots
    late = pl.pallas_call(
        functools.partial(late_kernel, n, first),
        out_shape=stage_outs(late_rows),
        in_specs=[smem, smem, smem, vmem, hbm, hbm],
        out_specs=[vmem] * (1 + half),
        scratch_shapes=[
            pltpu.VMEM(matrix.shape, matrix.dtype),
            pltpu.VMEM((n.blocks, n.width), f32),
            pltpu.VMEM(stage, f32),
            pltpu.SMEM((slots,), jnp.int32),
            pltpu.SemaphoreType.DMA((pieces,)),
        ],
        compiler_params=megabytes(
            (n.rows_dev, n.columns // 2), stage, sample_rows.shape, (n.grp_axis, n.rows_axis, late_rows, n.width)
        ),
        cost_estimate=pl.CostEstimate(
            flops=2 * slots * n.rows_dev * n.width * (n.width + n.samples) + 3 * matrix.size,
            transcendentals=0,
            bytes_accessed=2 * matrix.size,
        ),
        name="late_tiles",
    )(lists, pair_count, pairs, sample_rows, matrix, sent)

    halves = early_sums + reduce_scatter(late)[0]
    message = (n.cap * n.part + 2 * n.own, n.width)
    small = megabytes((4 * n.rows_axis,) + message)
    spread = pl.pallas_call(
        functools.partial(spread_kernel, n),
        out_shape=[jax.ShapeDtypeStruct(message, f32)] * n.rows_axis,
        in_specs=[vmem] * 6,
        out_specs=[vmem] * n.rows_axis,
        compiler_params=small,
        name="spread",
    )(*halves)
    came = [spread[0]] + [swap(spread[o], "rows", n.rows_axis, o) for o in range(1, n.rows_axis)]
    quarter = (n.own, n.part, n.width)
    *owned, total = pl.pallas_call(
        functools.partial(gather_kernel, n),
        out_shape=[jax.ShapeDtypeStruct(quarter, f32)] * n.grp_axis
        + [jax.ShapeDtypeStruct((2 * n.own, n.width), f32)],
        in_specs=[smem] + [vmem] * n.rows_axis,
        out_specs=[vmem] * (n.grp_axis + 1),
        scratch_shapes=[pltpu.VMEM((n.region, n.part, n.width), f32)],
        compiler_params=megabytes((n.rows_axis,) + message, (2 * n.grp_axis,) + quarter),
        name="gather",
    )(lists, *came)
    came = [owned[0]] + [
        swap(owned[d], "grp", n.grp_axis, d) for d in reversed(range(1, n.grp_axis))
    ][::-1]
    tiles = (n.own, n.width, n.width)
    factor = pl.pallas_call(
        functools.partial(factor_kernel, n),
        out_shape=jax.ShapeDtypeStruct(tiles, f32),
        in_specs=[vmem],
        out_specs=vmem,
        compiler_params=megabytes(tiles),
        name="factor",
    )(total)
    return pl.pallas_call(
        functools.partial(scale_kernel, n),
        out_shape=jax.ShapeDtypeStruct(tiles, f32),
        in_specs=[vmem] * (n.grp_axis + 1),
        out_specs=vmem,
        compiler_params=megabytes(tiles, tiles, tiles),
        name="scale",
    )(factor, *came)


def solution(mesh):
    in_specs = (P(("rows", "grp"), None), P(("rows", "grp"), None, None), P(), P(), P())
    out_specs = P(("rows", "grp"), None, None)

    def body(*args):
        return shards(mesh, *args)

    return jax.shard_map(body, mesh=mesh, in_specs=in_specs, out_specs=out_specs, check_vma=False)
```

profile of v0, /device:TPU:1, one launch (start us, length us, event | category | flops | bytes accessed | tf_op | source)
XLA Modules:
  0.0 68.2 jit_solution(2860000767968189710)
XLA Ops:
  0.0 0.9 %copy-done = s32[1,128,256]{2,1,0:T(8,128)S(1)} copy-done((s32[1,128,256]{2,1,0:T(8,128)S(1)}, s32[1,128,256]{2,1,0:T(8,128)}, u32[]{:S(2)}) %copy-start) | copy-done | bytes 131096
  0.9 0.7 %copy-done.2 = s32[8,8,4]{1,2,0:T(4,128)S(1)} copy-done((s32[8,8,4]{1,2,0:T(4,128)S(1)}, s32[8,8,4]{1,2,0:T(4,128)}, u32[]{:S(2)}) %copy-start.2) | copy-done | bytes 1048
  1.6 0.7 %copy-done.4 = s32[8,8]{1,0:T(8,128)S(1)} copy-done((s32[8,8]{1,0:T(8,128)S(1)}, s32[8,8]{1,0:T(8,128)}, u32[]{:S(2)}) %copy-start.4) | copy-done | bytes 280
  2.3 0.7 copy-done.6
  3.0 9.3 %early_tiles.1 = (f32[2,8,96,128]{3,2,1,0:T(8,128)S(1)}, f32[8,96,128]{2,1,0:T(8,128)S(1)}, f32[8,96,128]{2,1,0:T(8,128)S(1)}) custom-call(s32[8,4,8]{2,1,0:T(4,128)S(1)} %bitcast.10, s32[8,8]{1,0:T(8,128)S(1)} %copy-done.4, s32[2,256]{1,0:T(2,128)S(1)} %bitcast.13, s32[1,128,256]{2,1,0:T(8,128)S(1)} %copy-done, bf16[320,16384]{1,0:T(8,128)(2,1)} %matrix.3), custom_call_target="tpu_custom_call" | custom-call | tf_op jit(solution)/shard_map/early_tiles/pallas_call | solution.py:267
  12.3 0.1 collective-permute-start
  12.4 2.3 %collective-permute-done.refs_1_ = f32[2,8,96,128]{3,2,1,0:T(8,128)S(1)} collective-permute-done((f32[2,8,96,128]{3,2,1,0:T(8,128)S(1)}, f32[2,8,96,128]{3,2,1,0:T(8,128)S(1)}, u32[]{:S(2)}, u32[]{:S(2)}) %collective-permute-start) | collective-permute-done | bytes 786464 | tf_op jit(solution)/shard_map/ppermute | solution.py:240
  14.7 7.9 %late_tiles.1 = (f32[2,8,48,128]{3,2,1,0:T(8,128)S(1)}, f32[8,48,128]{2,1,0:T(8,128)S(1)}, f32[8,48,128]{2,1,0:T(8,128)S(1)}) custom-call(s32[8,4,8]{2,1,0:T(4,128)S(1)} %bitcast.11, s32[8,8]{1,0:T(8,128)S(1)} %copy-done.5, s32[2,256]{1,0:T(2,128)S(1)} %bitcast.14, s32[1,128,256]{2,1,0:T(8,128)S(1)} %copy-done.1, bf16[320,16384]{1,0:T(8,128)(2,1)} %matrix.3, ...), custom_call_target="tpu_custom_call" | custom-call | flops 267386880 | bytes 10485760 | tf_op jit(solution)/shard_map/late_tiles/pallas_call | solution.py:303
  22.7 0.2 collective-permute-start.2
  22.9 2.6 %collective-permute-start.1 = (f32[8,96,128]{2,1,0:T(8,128)S(1)}, f32[8,96,128]{2,1,0:T(8,128)S(1)}, u32[]{:S(2)}, u32[]{:S(2)}) collective-permute-start(f32[8,96,128]{2,1,0:T(8,128)S(1)} %fusion.after), channel_id=1, source_target_pairs={{0,2},{1,3},{2,0},{3,1},{4,6},{5,7},{6,4},{7,5},{8,10},{9,11},{10,... | collective-permute-start | bytes 1179656 | tf_op jit(solution)/shard_map/ppermute | solution.py:240
  25.5 0.0 collective-permute-done.2.refs_4_
  25.5 1.4 %collective-permute-start.3 = (f32[8,48,128]{2,1,0:T(8,128)S(1)}, f32[8,48,128]{2,1,0:T(8,128)S(1)}, u32[]{:S(2)}, u32[]{:S(2)}) collective-permute-start(f32[8,48,128]{2,1,0:T(8,128)S(1)} %fusion.1), channel_id=1, source_target_pairs={{0,2},{1,3},{2,0},{3,1},{4,6},{5,7},{6,4},{7,5},{8,10},{9,11},{10,... | collective-permute-start | bytes 589832 | tf_op jit(solution)/shard_map/ppermute | solution.py:240
  26.9 7.9 %collective-permute-done.1.refs_2_ = f32[8,96,128]{2,1,0:T(8,128)S(1)} collective-permute-done((f32[8,96,128]{2,1,0:T(8,128)S(1)}, f32[8,96,128]{2,1,0:T(8,128)S(1)}, u32[]{:S(2)}, u32[]{:S(2)}) %collective-permute-start.1) | collective-permute-done | bytes 393248 | tf_op jit(solution)/shard_map/ppermute | solution.py:240
  34.8 4.2 %collective-permute-done.3.refs_5_ = f32[8,48,128]{2,1,0:T(8,128)S(1)} collective-permute-done((f32[8,48,128]{2,1,0:T(8,128)S(1)}, f32[8,48,128]{2,1,0:T(8,128)S(1)}, u32[]{:S(2)}, u32[]{:S(2)}) %collective-permute-start.3) | collective-permute-done | bytes 196640 | tf_op jit(solution)/shard_map/ppermute | solution.py:240
  39.0 0.1 spread.1
  39.1 0.1 collective-permute-start.4
  39.2 1.3 %collective-permute-start.5 = (f32[144,128]{1,0:T(8,128)S(1)}, f32[144,128]{1,0:T(8,128)S(1)}, u32[]{:S(2)}, u32[]{:S(2)}) collective-permute-start(f32[144,128]{1,0:T(8,128)S(1)} %get-tuple-element.32), channel_id=1, source_target_pairs={{0,8},{4,12},{8,0},{12,4},{16,24},{20,28},{24,16},{28,20},{1,9},{5... | collective-permute-start | bytes 221192 | tf_op jit(solution)/shard_map/ppermute | solution.py:240
  40.5 1.3 %collective-permute-start.6 = (f32[144,128]{1,0:T(8,128)S(1)}, f32[144,128]{1,0:T(8,128)S(1)}, u32[]{:S(2)}, u32[]{:S(2)}) collective-permute-start(f32[144,128]{1,0:T(8,128)S(1)} %get-tuple-element.33), channel_id=1, source_target_pairs={{0,12},{4,8},{8,4},{12,0},{16,28},{20,24},{24,20},{28,16},{1,13},{... | collective-permute-start | bytes 221192 | tf_op jit(solution)/shard_map/ppermute | solution.py:240
  41.8 2.1 %collective-permute-start.7 = (f32[144,128]{1,0:T(8,128)S(1)}, f32[144,128]{1,0:T(8,128)S(1)}, u32[]{:S(2)}, u32[]{:S(2)}) collective-permute-start(f32[144,128]{1,0:T(8,128)S(1)} %get-tuple-element.34), channel_id=1, source_target_pairs={{0,16},{4,20},{8,24},{12,28},{16,0},{20,4},{24,8},{28,12},{1,17},{... | collective-permute-start | bytes 221192 | tf_op jit(solution)/shard_map/ppermute | solution.py:240
  43.9 0.9 %collective-permute-start.8 = (f32[144,128]{1,0:T(8,128)S(1)}, f32[144,128]{1,0:T(8,128)S(1)}, u32[]{:S(2)}, u32[]{:S(2)}) collective-permute-start(f32[144,128]{1,0:T(8,128)S(1)} %get-tuple-element.35), channel_id=1, source_target_pairs={{0,20},{4,16},{8,28},{12,24},{16,4},{20,0},{24,12},{28,8},{1,21},{... | collective-permute-start | bytes 221192 | tf_op jit(solution)/shard_map/ppermute | solution.py:240
  44.8 0.0 collective-permute-done.4.refs_1_
  44.9 3.5 %collective-permute-start.9 = (f32[144,128]{1,0:T(8,128)S(1)}, f32[144,128]{1,0:T(8,128)S(1)}, u32[]{:S(2)}, u32[]{:S(2)}) collective-permute-start(f32[144,128]{1,0:T(8,128)S(1)} %get-tuple-element.36), channel_id=1, source_target_pairs={{0,24},{4,28},{8,16},{12,20},{16,8},{20,12},{24,0},{28,4},{1,25},{... | collective-permute-start | bytes 221192 | tf_op jit(solution)/shard_map/ppermute | solution.py:240
  48.4 0.0 collective-permute-done.7.refs_4_
  48.4 6.6 %collective-permute-done.8.refs_5_ = f32[144,128]{1,0:T(8,128)S(1)} collective-permute-done((f32[144,128]{1,0:T(8,128)S(1)}, f32[144,128]{1,0:T(8,128)S(1)}, u32[]{:S(2)}, u32[]{:S(2)}) %collective-permute-start.8) | collective-permute-done | bytes 73760 | tf_op jit(solution)/shard_map/ppermute | solution.py:240
  55.0 1.0 %gather.1 = (f32[8,32,128]{2,1,0:T(8,128)S(1)}, f32[8,32,128]{2,1,0:T(8,128)S(1)}, f32[8,32,128]{2,1,0:T(8,128)S(1)}, f32[8,32,128]{2,1,0:T(8,128)S(1)}, f32[16,128]{1,0:T(8,128)S(1)}) custom-call(s32[8,4,8]{2,1,0:T(4,128)S(1)} %bitcast.12, f32[144,128]{1,0:T(8,128)S(1)} %get-tuple-element.30.refs_0_, f32[144,128]{1,0:T(8,128)S(1)} %collective-permute-done.4.refs_1_, ...), custom_call_target="tpu_custom_call" | custom-call | tf_op jit(solution)/shard_map/gather/pallas_call | solution.py:339
  56.1 3.2 %collective-permute-start.11 = (f32[8,32,128]{2,1,0:T(8,128)S(1)}, f32[8,32,128]{2,1,0:T(8,128)S(1)}, u32[]{:S(2)}, u32[]{:S(2)}) collective-permute-start(f32[8,32,128]{2,1,0:T(8,128)S(1)} %get-tuple-element.40), channel_id=1, source_target_pairs={{0,1},{1,0},{2,3},{3,2},{4,5},{5,4},{6,7},{7,6},{8,9},{9,8},{10,11... | collective-permute-start | bytes 393224 | tf_op jit(solution)/shard_map/ppermute | solution.py:240
  59.3 1.2 %collective-permute-start.12 = (f32[8,32,128]{2,1,0:T(8,128)S(1)}, f32[8,32,128]{2,1,0:T(8,128)S(1)}, u32[]{:S(2)}, u32[]{:S(2)}) collective-permute-start(f32[8,32,128]{2,1,0:T(8,128)S(1)} %get-tuple-element.41), channel_id=1, source_target_pairs={{0,2},{1,3},{2,0},{3,1},{4,6},{5,7},{6,4},{7,5},{8,10},{9,11},{10,... | collective-permute-start | bytes 393224 | tf_op jit(solution)/shard_map/ppermute | solution.py:240
  60.6 0.5 collective-permute-start.13
  61.0 0.2 factor.1
  61.3 3.0 %collective-permute-done.12.refs_2_ = f32[8,32,128]{2,1,0:T(8,128)S(1)} collective-permute-done((f32[8,32,128]{2,1,0:T(8,128)S(1)}, f32[8,32,128]{2,1,0:T(8,128)S(1)}, u32[]{:S(2)}, u32[]{:S(2)}) %collective-permute-start.12) | collective-permute-done | bytes 131104 | tf_op jit(solution)/shard_map/ppermute | solution.py:240
  64.3 3.1 %collective-permute-done.13.refs_3_ = f32[8,32,128]{2,1,0:T(8,128)S(1)} collective-permute-done((f32[8,32,128]{2,1,0:T(8,128)S(1)}, f32[8,32,128]{2,1,0:T(8,128)S(1)}, u32[]{:S(2)}, u32[]{:S(2)}) %collective-permute-start.13) | collective-permute-done | bytes 131104 | tf_op jit(solution)/shard_map/ppermute | solution.py:240
  67.4 0.8 %scale.1 = f32[8,128,128]{2,1,0:T(8,128)} custom-call(f32[8,128,128]{2,1,0:T(8,128)S(1)} %factor.1, f32[8,32,128]{2,1,0:T(8,128)S(1)} %get-tuple-element.39.refs_0_, f32[8,32,128]{2,1,0:T(8,128)S(1)} %collective-permute-done.11.refs_1_, f32[8,32,128]{2,1,0:T(8,128)S(1)} %collective-permute-done.12.refs_2_, f32[8,32,128]{2,1,0:T(8,128)S(1)} %collective-permute-done.13.refs_3_), custom_call_target="tpu_custom_call" | custom-call | tf_op jit(solution)/shard_map/scale/pallas_call | solution.py:361
  (20 shorter events, 0.1 us)
Async XLA Ops:
  0.0 14.7 %copy-start.7 = (s32[256,2]{0,1:T(2,128)S(1)}, s32[256,2]{0,1:T(2,128)}, u32[]{:S(2)}) copy-start(s32[256,2]{0,1:T(2,128)} %param.9) | copy-start | bytes 6148
  0.0 0.9 %copy-start = (s32[1,128,256]{2,1,0:T(8,128)S(1)}, s32[1,128,256]{2,1,0:T(8,128)}, u32[]{:S(2)}) copy-start(s32[1,128,256]{2,1,0:T(8,128)} %samples.3) | copy-start | bytes 393220
  0.9 0.7 %copy-start.2 = (s32[8,8,4]{1,2,0:T(4,128)S(1)}, s32[8,8,4]{1,2,0:T(4,128)}, u32[]{:S(2)}) copy-start(s32[8,8,4]{1,2,0:T(4,128)} %param.7) | copy-start | bytes 3076
  1.6 0.7 %copy-start.4 = (s32[8,8]{1,0:T(8,128)S(1)}, s32[8,8]{1,0:T(8,128)}, u32[]{:S(2)}) copy-start(s32[8,8]{1,0:T(8,128)} %counts.3) | copy-start | bytes 772
  2.3 0.7 copy-start.6
  3.0 11.7 %copy-start.1 = (s32[1,128,256]{2,1,0:T(8,128)S(1)}, s32[1,128,256]{2,1,0:T(8,128)}, u32[]{:S(2)}) copy-start(s32[1,128,256]{2,1,0:T(8,128)} %samples.3) | copy-start | bytes 393220
  3.0 11.7 %copy-start.3 = (s32[8,8,4]{1,2,0:T(4,128)S(1)}, s32[8,8,4]{1,2,0:T(4,128)}, u32[]{:S(2)}) copy-start(s32[8,8,4]{1,2,0:T(4,128)} %param.7) | copy-start | bytes 3076
  3.0 11.7 %copy-start.5 = (s32[8,8]{1,0:T(8,128)S(1)}, s32[8,8]{1,0:T(8,128)}, u32[]{:S(2)}) copy-start(s32[8,8]{1,0:T(8,128)} %counts.3) | copy-start | bytes 772
  12.3 2.4 %collective-permute-start = (f32[2,8,96,128]{3,2,1,0:T(8,128)S(1)}, f32[2,8,96,128]{3,2,1,0:T(8,128)S(1)}, u32[]{:S(2)}, u32[]{:S(2)}) collective-permute-start(f32[2,8,96,128]{3,2,1,0:T(8,128)S(1)} %get-tuple-element.25), channel_id=1, source_target_pairs={{0,1},{1,0},{2,3},{3,2},{4,5},{5,4},{6,7},{7,6},{8,9},{9,8},{10,11... | collective-permute-start | bytes 2359304 | tf_op jit(solution)/shard_map/ppermute | solution.py:240
  22.7 2.8 %collective-permute-start.2 = (f32[2,8,48,128]{3,2,1,0:T(8,128)S(1)}, f32[2,8,48,128]{3,2,1,0:T(8,128)S(1)}, u32[]{:S(2)}, u32[]{:S(2)}) collective-permute-start(f32[2,8,48,128]{3,2,1,0:T(8,128)S(1)} %get-tuple-element.28), channel_id=1, source_target_pairs={{0,1},{1,0},{2,3},{3,2},{4,5},{5,4},{6,7},{7,6},{8,9},{9,8},{10,11... | collective-permute-start | bytes 1179656 | tf_op jit(solution)/shard_map/ppermute | solution.py:240
  22.9 12.0 %collective-permute-start.1 = (f32[8,96,128]{2,1,0:T(8,128)S(1)}, f32[8,96,128]{2,1,0:T(8,128)S(1)}, u32[]{:S(2)}, u32[]{:S(2)}) collective-permute-start(f32[8,96,128]{2,1,0:T(8,128)S(1)} %fusion.after), channel_id=1, source_target_pairs={{0,2},{1,3},{2,0},{3,1},{4,6},{5,7},{6,4},{7,5},{8,10},{9,11},{10,... | collective-permute-start | bytes 1179656 | tf_op jit(solution)/shard_map/ppermute | solution.py:240
  25.5 13.5 %collective-permute-start.3 = (f32[8,48,128]{2,1,0:T(8,128)S(1)}, f32[8,48,128]{2,1,0:T(8,128)S(1)}, u32[]{:S(2)}, u32[]{:S(2)}) collective-permute-start(f32[8,48,128]{2,1,0:T(8,128)S(1)} %fusion.1), channel_id=1, source_target_pairs={{0,2},{1,3},{2,0},{3,1},{4,6},{5,7},{6,4},{7,5},{8,10},{9,11},{10,... | collective-permute-start | bytes 589832 | tf_op jit(solution)/shard_map/ppermute | solution.py:240
  39.1 5.7 %collective-permute-start.4 = (f32[144,128]{1,0:T(8,128)S(1)}, f32[144,128]{1,0:T(8,128)S(1)}, u32[]{:S(2)}, u32[]{:S(2)}) collective-permute-start(f32[144,128]{1,0:T(8,128)S(1)} %get-tuple-element.31), channel_id=1, source_target_pairs={{0,4},{4,0},{8,12},{12,8},{16,20},{20,16},{24,28},{28,24},{1,5},{5... | collective-permute-start | bytes 221192 | tf_op jit(solution)/shard_map/ppermute | solution.py:240
  39.2 9.2 %collective-permute-start.5 = (f32[144,128]{1,0:T(8,128)S(1)}, f32[144,128]{1,0:T(8,128)S(1)}, u32[]{:S(2)}, u32[]{:S(2)}) collective-permute-start(f32[144,128]{1,0:T(8,128)S(1)} %get-tuple-element.32), channel_id=1, source_target_pairs={{0,8},{4,12},{8,0},{12,4},{16,24},{20,28},{24,16},{28,20},{1,9},{5... | collective-permute-start | bytes 221192 | tf_op jit(solution)/shard_map/ppermute | solution.py:240
  40.5 7.9 %collective-permute-start.6 = (f32[144,128]{1,0:T(8,128)S(1)}, f32[144,128]{1,0:T(8,128)S(1)}, u32[]{:S(2)}, u32[]{:S(2)}) collective-permute-start(f32[144,128]{1,0:T(8,128)S(1)} %get-tuple-element.33), channel_id=1, source_target_pairs={{0,12},{4,8},{8,4},{12,0},{16,28},{20,24},{24,20},{28,16},{1,13},{... | collective-permute-start | bytes 221192 | tf_op jit(solution)/shard_map/ppermute | solution.py:240
  41.8 6.6 %collective-permute-start.7 = (f32[144,128]{1,0:T(8,128)S(1)}, f32[144,128]{1,0:T(8,128)S(1)}, u32[]{:S(2)}, u32[]{:S(2)}) collective-permute-start(f32[144,128]{1,0:T(8,128)S(1)} %get-tuple-element.34), channel_id=1, source_target_pairs={{0,16},{4,20},{8,24},{12,28},{16,0},{20,4},{24,8},{28,12},{1,17},{... | collective-permute-start | bytes 221192 | tf_op jit(solution)/shard_map/ppermute | solution.py:240
  43.9 11.1 %collective-permute-start.8 = (f32[144,128]{1,0:T(8,128)S(1)}, f32[144,128]{1,0:T(8,128)S(1)}, u32[]{:S(2)}, u32[]{:S(2)}) collective-permute-start(f32[144,128]{1,0:T(8,128)S(1)} %get-tuple-element.35), channel_id=1, source_target_pairs={{0,20},{4,16},{8,28},{12,24},{16,4},{20,0},{24,12},{28,8},{1,21},{... | collective-permute-start | bytes 221192 | tf_op jit(solution)/shard_map/ppermute | solution.py:240
  44.9 10.2 %collective-permute-start.9 = (f32[144,128]{1,0:T(8,128)S(1)}, f32[144,128]{1,0:T(8,128)S(1)}, u32[]{:S(2)}, u32[]{:S(2)}) collective-permute-start(f32[144,128]{1,0:T(8,128)S(1)} %get-tuple-element.36), channel_id=1, source_target_pairs={{0,24},{4,28},{8,16},{12,20},{16,8},{20,12},{24,0},{28,4},{1,25},{... | collective-permute-start | bytes 221192 | tf_op jit(solution)/shard_map/ppermute | solution.py:240
  48.4 6.7 %collective-permute-start.10 = (f32[144,128]{1,0:T(8,128)S(1)}, f32[144,128]{1,0:T(8,128)S(1)}, u32[]{:S(2)}, u32[]{:S(2)}) collective-permute-start(f32[144,128]{1,0:T(8,128)S(1)} %get-tuple-element.37), channel_id=1, source_target_pairs={{0,28},{4,24},{8,20},{12,16},{16,12},{20,8},{24,4},{28,0},{1,29},{... | collective-permute-start | bytes 221192 | tf_op jit(solution)/shard_map/ppermute | solution.py:240
  56.1 5.2 %collective-permute-start.11 = (f32[8,32,128]{2,1,0:T(8,128)S(1)}, f32[8,32,128]{2,1,0:T(8,128)S(1)}, u32[]{:S(2)}, u32[]{:S(2)}) collective-permute-start(f32[8,32,128]{2,1,0:T(8,128)S(1)} %get-tuple-element.40), channel_id=1, source_target_pairs={{0,1},{1,0},{2,3},{3,2},{4,5},{5,4},{6,7},{7,6},{8,9},{9,8},{10,11... | collective-permute-start | bytes 393224 | tf_op jit(solution)/shard_map/ppermute | solution.py:240
  59.3 5.0 %collective-permute-start.12 = (f32[8,32,128]{2,1,0:T(8,128)S(1)}, f32[8,32,128]{2,1,0:T(8,128)S(1)}, u32[]{:S(2)}, u32[]{:S(2)}) collective-permute-start(f32[8,32,128]{2,1,0:T(8,128)S(1)} %get-tuple-element.41), channel_id=1, source_target_pairs={{0,2},{1,3},{2,0},{3,1},{4,6},{5,7},{6,4},{7,5},{8,10},{9,11},{10,... | collective-permute-start | bytes 393224 | tf_op jit(solution)/shard_map/ppermute | solution.py:240
  60.6 6.8 %collective-permute-start.13 = (f32[8,32,128]{2,1,0:T(8,128)S(1)}, f32[8,32,128]{2,1,0:T(8,128)S(1)}, u32[]{:S(2)}, u32[]{:S(2)}) collective-permute-start(f32[8,32,128]{2,1,0:T(8,128)S(1)} %get-tuple-element.42), channel_id=1, source_target_pairs={{0,3},{1,2},{2,1},{3,0},{4,7},{5,6},{6,5},{7,4},{8,11},{9,10},{10,... | collective-permute-start | bytes 393224 | tf_op jit(solution)/shard_map/ppermute | solution.py:240
where the time goes:
time: 68.6 us; the launch traced here: 68.2 us
  waiting for transfers between devices  27.1 us (40%)
  Pallas kernels  19.4 us (28%)
  starting transfers between devices  18.5 us (27%)
  local copies, waits for them, and re-layouts  3.02 us (4%)
    ppermute x14, waiting for transfers between devices, swap(): return lax.ppermute(x, axis, [(i, i ^ distance) for i in range(size)])  27.1 us
    ppermute x14, starting transfers between devices, swap(): return lax.ppermute(x, axis, [(i, i ^ distance) for i in range(size)])  18.5 us
    pallas_call x1, Pallas kernels, shards(): pl.pallas_call(functools.partial(early_kernel, n, first), out_shape=stage...  9.26 us
    pallas_call x1, Pallas kernels, shards(): pl.pallas_call(functools.partial(late_kernel, n, first), out_shape=stage_...  7.92 us
    unnamed x16, local copies, waits for them, and re-layouts  3.02 us
  transfers between devices with their start and end apart: 14, of which 6 were waited for; matrix products, arithmetic and copies ran while one was open for 0% of the time, Pallas kernels for 0%

commit v1 on v0

--- a/solution.py
+++ b/solution.py
@@ -9,7 +9,6 @@
 
 epsilon = 1e-06
 unroll = 4
-pieces = 16
 late_slots = 1
 
 
@@ -48,11 +47,9 @@
 def multiply(n, first, slots, loads, samples, blocks_of, stage, outs):
     g = lax.axis_index("grp")
     positions = lax.broadcasted_iota(jnp.int32, (n.rows_dev, n.samples), 0)
-    ones = jnp.ones((n.samples, n.width), jnp.bfloat16)
     for u, t in enumerate(slots):
-        drawn = samples[0, pl.ds(blocks_of(t)[0], 1), :]
-        hit = jnp.where(drawn == positions, 1.0, 0.0).astype(jnp.bfloat16)
-        times = jnp.dot(hit, ones, preferred_element_type=jnp.float32)
+        drawn = samples[pl.ds(blocks_of(t)[0], 1), :]
+        times = jnp.sum(jnp.where(drawn == positions, 1.0, 0.0), axis=1, keepdims=True)
         left, right = loads(u, t)
         weighted = (times * left.astype(jnp.float32)).astype(jnp.bfloat16)
         stage[u] = lax.dot_general(
@@ -83,8 +80,10 @@
 
 def early_kernel(n, last, lists, counts, pairs, samples, matrix, *rest):
     outs = split_outs(n, rest[: 1 + n.grp_axis // 2])
-    held, stage, live, arrive = rest[1 + n.grp_axis // 2 :]
+    held, drawn, stage, live, arrive, came = rest[1 + n.grp_axis // 2 :]
     me = lax.axis_index("rows")
+    draws = pltpu.make_async_copy(samples.at[0], drawn, came)
+    draws.start()
 
     def blocks_of(t):
         pair = lists[me, t % n.cap, jnp.bitwise_xor(t // n.cap, me)]
@@ -110,6 +109,7 @@
 
     lax.fori_loop(0, found, begin, 0)
     clear(outs, n, last * n.part)
+    draws.wait()
 
     def group(i, carry):
         at = [jnp.where(i * unroll + u < found, i * unroll + u, 0) for u in range(unroll)]
@@ -124,7 +124,7 @@
         def loads(u, t):
             return held[at[u], 0], held[at[u], 1]
 
-        multiply(n, 0, slots, loads, samples, blocks_of, stage, outs)
+        multiply(n, 0, slots, loads, drawn, blocks_of, stage, outs)
         return carry
 
     lax.fori_loop(0, pl.cdiv(found, unroll), group, 0)
@@ -132,33 +132,22 @@
 
 def late_kernel(n, first, lists, counts, pairs, samples, matrix, after, *rest):
     outs = split_outs(n, rest[: 1 + n.grp_axis // 2])
-    local, sums, stage, live, arrive = rest[1 + n.grp_axis // 2 :]
+    sums, stage, live = rest[1 + n.grp_axis // 2 :]
     me = lax.axis_index("rows")
     g = lax.axis_index("grp")
-    piece_blocks = n.blocks // pieces
-    piece = piece_blocks * n.width
     tile_rows = (n.cap - first) * n.part
-
-    def copy(i):
-        span = pl.ds(i * piece, piece)
-        return pltpu.make_async_copy(matrix.at[:, span], local.at[:, span], arrive.at[i])
-
-    for i in range(pieces):
-        copy(i).start()
     found = list_live(n, first, n.cap, live, counts)
     clear(outs, n, tile_rows)
 
     def columns(b):
-        return local[:, pl.ds(pl.multiple_of(b * n.width, n.width), n.width)]
+        return matrix[:, pl.ds(pl.multiple_of(b * n.width, n.width), n.width)]
 
     def block_sum(b, carry):
         x = columns(b).astype(jnp.float32)
         sums[pl.ds(b, 1), :] = jnp.sum(x * x, axis=0, keepdims=True)
         return carry
 
-    for i in range(pieces):
-        copy(i).wait()
-        lax.fori_loop(i * piece_blocks, (i + 1) * piece_blocks, block_sum, 0, unroll=2)
+    lax.fori_loop(0, n.blocks, block_sum, 0, unroll=4)
 
     for d in range(n.grp_axis):
 
@@ -183,7 +172,7 @@
             both = blocks_of(t)
             return columns(both[0]), columns(both[1])
 
-        multiply(n, first, slots, loads, samples, blocks_of, stage, outs)
+        multiply(n, first, slots, loads, samples.at[0], blocks_of, stage, outs)
         return carry
 
     lax.fori_loop(0, pl.cdiv(found, unroll), group, 0)
@@ -251,9 +240,10 @@
     vmem = pl.BlockSpec(memory_space=pltpu.VMEM)
     smem = pl.BlockSpec(memory_space=pltpu.SMEM)
     hbm = pl.BlockSpec(memory_space=pl.ANY)
-    matrix = pltpu.with_memory_space_constraint(matrix, pltpu.HBM)
-    lists = jnp.transpose(pair_list, (0, 2, 1))
-    pairs = jnp.transpose(pair_blocks)
+    stay = functools.partial(pltpu.with_memory_space_constraint, memory_space=pltpu.HBM)
+    lists = stay(jnp.transpose(pair_list, (0, 2, 1)))
+    pairs = stay(jnp.transpose(pair_blocks))
+    pair_count = stay(pair_count)
     half = n.grp_axis // 2
     first = n.cap - late_slots
 
@@ -267,19 +257,21 @@
     early = pl.pallas_call(
         functools.partial(early_kernel, n, first),
         out_shape=stage_outs(rows),
-        in_specs=[smem, smem, smem, vmem, hbm],
+        in_specs=[smem, smem, smem, hbm, hbm],
         out_specs=[vmem] * (1 + half),
         scratch_shapes=[
             pltpu.VMEM((slots, 2, n.rows_dev, n.width), matrix.dtype),
+            pltpu.VMEM(sample_rows.shape[1:], jnp.int32),
             pltpu.VMEM(stage, f32),
             pltpu.SMEM((slots,), jnp.int32),
             pltpu.SemaphoreType.DMA((slots,)),
+            pltpu.SemaphoreType.DMA,
         ],
         compiler_params=megabytes(
             (slots, n.rows_dev, n.width), stage, sample_rows.shape, (n.grp_axis, n.rows_axis, rows, n.width)
         ),
         name="early_tiles",
-    )(lists, pair_count, pairs, sample_rows, matrix)
+    )(lists, pair_count, pairs, stay(sample_rows), stay(matrix))
 
     def reduce_scatter(outs):
         got = swap(outs[0], "grp", n.grp_axis, 1)
@@ -303,17 +295,15 @@
     late = pl.pallas_call(
         functools.partial(late_kernel, n, first),
         out_shape=stage_outs(late_rows),
-        in_specs=[smem, smem, smem, vmem, hbm, hbm],
+        in_specs=[smem, smem, smem, vmem, vmem, hbm],
         out_specs=[vmem] * (1 + half),
         scratch_shapes=[
-            pltpu.VMEM(matrix.shape, matrix.dtype),
             pltpu.VMEM((n.blocks, n.width), f32),
             pltpu.VMEM(stage, f32),
             pltpu.SMEM((slots,), jnp.int32),
-            pltpu.SemaphoreType.DMA((pieces,)),
         ],
         compiler_params=megabytes(
-            (n.rows_dev, n.columns // 2), stage, sample_rows.shape, (n.grp_axis, n.rows_axis, late_rows, n.width)
+            stage, (n.blocks, n.width), sample_rows.shape, (n.grp_axis, n.rows_axis, late_rows, n.width)
         ),
         cost_estimate=pl.CostEstimate(
             flops=2 * slots * n.rows_dev * n.width * (n.width + n.samples) + 3 * matrix.size,
@@ -334,7 +324,9 @@
         compiler_params=small,
         name="spread",
     )(*halves)
-    came = [spread[0]] + [swap(spread[o], "rows", n.rows_axis, o) for o in range(1, n.rows_axis)]
+    came = [spread[0]]
+    for o in range(1, n.rows_axis):
+        came.append(swap(spread[o], "rows", n.rows_axis, o))
     quarter = (n.own, n.part, n.width)
     *owned, total = pl.pallas_call(
         functools.partial(gather_kernel, n),

time: 68.6 us -> 61.4 us (0.90)
  Pallas kernels: 19.4 us -> 15.1 us
  local copies, waits for them, and re-layouts: 3.02 us -> 0.01 us
    unnamed x16 -> x4, local copies, waits for them, and re-layouts: 3.02 us -> 0.01 us
    pallas_call x1, Pallas kernels: 9.26 us -> 6.76 us  [shards(): pl.pallas_call(functools.partial(early_kernel, n, first), out_shape=stage...]
    pallas_call x1, Pallas kernels: 7.92 us -> 6.05 us  [shards(): pl.pallas_call(functools.partial(late_kernel, n, first), out_shape=stage_...]
where the time goes in v1:
time: 61.4 us; the launch traced here: 60.9 us
  waiting for transfers between devices  27.1 us (44%)
  starting transfers between devices  18.5 us (30%)
  Pallas kernels  15.1 us (25%)
    ppermute x14, waiting for transfers between devices, swap(): return lax.ppermute(x, axis, [(i, i ^ distance) for i in range(size)])  27.1 us
    ppermute x14, starting transfers between devices, swap(): return lax.ppermute(x, axis, [(i, i ^ distance) for i in range(size)])  18.5 us
    pallas_call x1, Pallas kernels, shards(): pl.pallas_call(functools.partial(early_kernel, n, first), out_shape=stage...  6.76 us
    pallas_call x1, Pallas kernels, shards(): pl.pallas_call(functools.partial(late_kernel, n, first), out_shape=stage_...  6.05 us
  transfers between devices with their start and end apart: 14, of which 6 were waited for; matrix products, arithmetic and copies ran while one was open for 0% of the time, Pallas kernels for 0%

profile of v1, /device:TPU:1, one launch (start us, length us, event | category | flops | bytes accessed | tf_op | source)
XLA Modules:
  0.0 60.9 jit_solution(7772157671447662379)
XLA Ops:
  0.0 6.8 %early_tiles.1 = (f32[2,8,96,128]{3,2,1,0:T(8,128)S(1)}, f32[8,96,128]{2,1,0:T(8,128)S(1)}, f32[8,96,128]{2,1,0:T(8,128)S(1)}) custom-call(s32[8,4,8]{2,1,0:T(4,128)} %bitcast.10, s32[8,8]{1,0:T(8,128)} %counts.3, s32[2,256]{1,0:T(2,128)} %bitcast.13, s32[1,128,256]{2,1,0:T(8,128)} %samples.3, bf16[320,16384]{1,0:T(8,128)(2,1)} %matrix.3), custom_call_target="tpu_custom_call" | custom-call | tf_op jit(solution)/shard_map/early_tiles/pallas_call | solution.py:257
  6.8 0.1 collective-permute-start
  6.9 2.3 %collective-permute-done.refs_1_ = f32[2,8,96,128]{3,2,1,0:T(8,128)S(1)} collective-permute-done((f32[2,8,96,128]{3,2,1,0:T(8,128)S(1)}, f32[2,8,96,128]{3,2,1,0:T(8,128)S(1)}, u32[]{:S(2)}, u32[]{:S(2)}) %collective-permute-start) | collective-permute-done | bytes 786464 | tf_op jit(solution)/shard_map/ppermute | solution.py:229
  9.2 6.1 %late_tiles.1 = (f32[2,8,48,128]{3,2,1,0:T(8,128)S(1)}, f32[8,48,128]{2,1,0:T(8,128)S(1)}, f32[8,48,128]{2,1,0:T(8,128)S(1)}) custom-call(s32[8,4,8]{2,1,0:T(4,128)} %bitcast.11, s32[8,8]{1,0:T(8,128)} %counts.3, s32[2,256]{1,0:T(2,128)} %bitcast.14, s32[1,128,256]{2,1,0:T(8,128)S(1)} %copy-done.1, bf16[320,16384]{1,0:T(8,128)(2,1)S(1)} %copy-done, ...), custom_call_target="tpu_custom_call" | custom-call | flops 267386880 | bytes 10485760 | tf_op jit(solution)/shard_map/late_tiles/pallas_call | solution.py:295
  15.3 0.2 collective-permute-start.2
  15.5 2.6 %collective-permute-start.1 = (f32[8,96,128]{2,1,0:T(8,128)S(1)}, f32[8,96,128]{2,1,0:T(8,128)S(1)}, u32[]{:S(2)}, u32[]{:S(2)}) collective-permute-start(f32[8,96,128]{2,1,0:T(8,128)S(1)} %fusion.after), channel_id=1, source_target_pairs={{0,2},{1,3},{2,0},{3,1},{4,6},{5,7},{6,4},{7,5},{8,10},{9,11},{10,... | collective-permute-start | bytes 1179656 | tf_op jit(solution)/shard_map/ppermute | solution.py:229
  18.1 0.0 collective-permute-done.2.refs_4_
  18.1 1.4 %collective-permute-start.3 = (f32[8,48,128]{2,1,0:T(8,128)S(1)}, f32[8,48,128]{2,1,0:T(8,128)S(1)}, u32[]{:S(2)}, u32[]{:S(2)}) collective-permute-start(f32[8,48,128]{2,1,0:T(8,128)S(1)} %fusion.1), channel_id=1, source_target_pairs={{0,2},{1,3},{2,0},{3,1},{4,6},{5,7},{6,4},{7,5},{8,10},{9,11},{10,... | collective-permute-start | bytes 589832 | tf_op jit(solution)/shard_map/ppermute | solution.py:229
  19.5 7.9 %collective-permute-done.1.refs_2_ = f32[8,96,128]{2,1,0:T(8,128)S(1)} collective-permute-done((f32[8,96,128]{2,1,0:T(8,128)S(1)}, f32[8,96,128]{2,1,0:T(8,128)S(1)}, u32[]{:S(2)}, u32[]{:S(2)}) %collective-permute-start.1) | collective-permute-done | bytes 393248 | tf_op jit(solution)/shard_map/ppermute | solution.py:229
  27.4 4.2 %collective-permute-done.3.refs_5_ = f32[8,48,128]{2,1,0:T(8,128)S(1)} collective-permute-done((f32[8,48,128]{2,1,0:T(8,128)S(1)}, f32[8,48,128]{2,1,0:T(8,128)S(1)}, u32[]{:S(2)}, u32[]{:S(2)}) %collective-permute-start.3) | collective-permute-done | bytes 196640 | tf_op jit(solution)/shard_map/ppermute | solution.py:229
  31.6 0.1 spread.1
  31.7 0.1 collective-permute-start.4
  31.8 1.8 %collective-permute-start.5 = (f32[144,128]{1,0:T(8,128)S(1)}, f32[144,128]{1,0:T(8,128)S(1)}, u32[]{:S(2)}, u32[]{:S(2)}) collective-permute-start(f32[144,128]{1,0:T(8,128)S(1)} %get-tuple-element.32), channel_id=1, source_target_pairs={{0,8},{4,12},{8,0},{12,4},{16,24},{20,28},{24,16},{28,20},{1,9},{5... | collective-permute-start | bytes 221192 | tf_op jit(solution)/shard_map/ppermute | solution.py:229
  33.6 0.8 %collective-permute-start.6 = (f32[144,128]{1,0:T(8,128)S(1)}, f32[144,128]{1,0:T(8,128)S(1)}, u32[]{:S(2)}, u32[]{:S(2)}) collective-permute-start(f32[144,128]{1,0:T(8,128)S(1)} %get-tuple-element.33), channel_id=1, source_target_pairs={{0,12},{4,8},{8,4},{12,0},{16,28},{20,24},{24,20},{28,16},{1,13},{... | collective-permute-start | bytes 221192 | tf_op jit(solution)/shard_map/ppermute | solution.py:229
  34.5 2.1 %collective-permute-start.7 = (f32[144,128]{1,0:T(8,128)S(1)}, f32[144,128]{1,0:T(8,128)S(1)}, u32[]{:S(2)}, u32[]{:S(2)}) collective-permute-start(f32[144,128]{1,0:T(8,128)S(1)} %get-tuple-element.34), channel_id=1, source_target_pairs={{0,16},{4,20},{8,24},{12,28},{16,0},{20,4},{24,8},{28,12},{1,17},{... | collective-permute-start | bytes 221192 | tf_op jit(solution)/shard_map/ppermute | solution.py:229
  36.6 0.9 %collective-permute-start.8 = (f32[144,128]{1,0:T(8,128)S(1)}, f32[144,128]{1,0:T(8,128)S(1)}, u32[]{:S(2)}, u32[]{:S(2)}) collective-permute-start(f32[144,128]{1,0:T(8,128)S(1)} %get-tuple-element.35), channel_id=1, source_target_pairs={{0,20},{4,16},{8,28},{12,24},{16,4},{20,0},{24,12},{28,8},{1,21},{... | collective-permute-start | bytes 221192 | tf_op jit(solution)/shard_map/ppermute | solution.py:229
  37.5 0.0 collective-permute-done.4.refs_1_
  37.5 3.5 %collective-permute-start.9 = (f32[144,128]{1,0:T(8,128)S(1)}, f32[144,128]{1,0:T(8,128)S(1)}, u32[]{:S(2)}, u32[]{:S(2)}) collective-permute-start(f32[144,128]{1,0:T(8,128)S(1)} %get-tuple-element.36), channel_id=1, source_target_pairs={{0,24},{4,28},{8,16},{12,20},{16,8},{20,12},{24,0},{28,4},{1,25},{... | collective-permute-start | bytes 221192 | tf_op jit(solution)/shard_map/ppermute | solution.py:229
  41.0 0.0 collective-permute-done.5.refs_2_
  41.0 0.0 collective-permute-start.10
  41.0 0.0 collective-permute-done.7.refs_4_
  41.0 6.6 %collective-permute-done.8.refs_5_ = f32[144,128]{1,0:T(8,128)S(1)} collective-permute-done((f32[144,128]{1,0:T(8,128)S(1)}, f32[144,128]{1,0:T(8,128)S(1)}, u32[]{:S(2)}, u32[]{:S(2)}) %collective-permute-start.8) | collective-permute-done | bytes 73760 | tf_op jit(solution)/shard_map/ppermute | solution.py:229
  47.7 0.0 collective-permute-done.10.refs_7_
  47.7 1.1 %gather.1 = (f32[8,32,128]{2,1,0:T(8,128)S(1)}, f32[8,32,128]{2,1,0:T(8,128)S(1)}, f32[8,32,128]{2,1,0:T(8,128)S(1)}, f32[8,32,128]{2,1,0:T(8,128)S(1)}, f32[16,128]{1,0:T(8,128)S(1)}) custom-call(s32[8,4,8]{2,1,0:T(4,128)} %bitcast.12, f32[144,128]{1,0:T(8,128)S(1)} %get-tuple-element.30.refs_0_, f32[144,128]{1,0:T(8,128)S(1)} %collective-permute-done.4.refs_1_, ...), custom_call_target="tpu_custom_call" | custom-call | tf_op jit(solution)/shard_map/gather/pallas_call | solution.py:331
  48.8 3.2 %collective-permute-start.11 = (f32[8,32,128]{2,1,0:T(8,128)S(1)}, f32[8,32,128]{2,1,0:T(8,128)S(1)}, u32[]{:S(2)}, u32[]{:S(2)}) collective-permute-start(f32[8,32,128]{2,1,0:T(8,128)S(1)} %get-tuple-element.40), channel_id=1, source_target_pairs={{0,1},{1,0},{2,3},{3,2},{4,5},{5,4},{6,7},{7,6},{8,9},{9,8},{10,11... | collective-permute-start | bytes 393224 | tf_op jit(solution)/shard_map/ppermute | solution.py:229
  52.1 1.2 %collective-permute-start.12 = (f32[8,32,128]{2,1,0:T(8,128)S(1)}, f32[8,32,128]{2,1,0:T(8,128)S(1)}, u32[]{:S(2)}, u32[]{:S(2)}) collective-permute-start(f32[8,32,128]{2,1,0:T(8,128)S(1)} %get-tuple-element.41), channel_id=1, source_target_pairs={{0,2},{1,3},{2,0},{3,1},{4,6},{5,7},{6,4},{7,5},{8,10},{9,11},{10,... | collective-permute-start | bytes 393224 | tf_op jit(solution)/shard_map/ppermute | solution.py:229
  53.3 0.5 collective-permute-start.13
  53.8 0.2 factor.1
  54.0 0.0 collective-permute-done.11.refs_1_
  54.0 3.0 %collective-permute-done.12.refs_2_ = f32[8,32,128]{2,1,0:T(8,128)S(1)} collective-permute-done((f32[8,32,128]{2,1,0:T(8,128)S(1)}, f32[8,32,128]{2,1,0:T(8,128)S(1)}, u32[]{:S(2)}, u32[]{:S(2)}) %collective-permute-start.12) | collective-permute-done | bytes 131104 | tf_op jit(solution)/shard_map/ppermute | solution.py:229
  57.0 3.1 %collective-permute-done.13.refs_3_ = f32[8,32,128]{2,1,0:T(8,128)S(1)} collective-permute-done((f32[8,32,128]{2,1,0:T(8,128)S(1)}, f32[8,32,128]{2,1,0:T(8,128)S(1)}, u32[]{:S(2)}, u32[]{:S(2)}) %collective-permute-start.13) | collective-permute-done | bytes 131104 | tf_op jit(solution)/shard_map/ppermute | solution.py:229
  60.1 0.8 %scale.1 = f32[8,128,128]{2,1,0:T(8,128)} custom-call(f32[8,128,128]{2,1,0:T(8,128)S(1)} %factor.1, f32[8,32,128]{2,1,0:T(8,128)S(1)} %get-tuple-element.39.refs_0_, f32[8,32,128]{2,1,0:T(8,128)S(1)} %collective-permute-done.11.refs_1_, f32[8,32,128]{2,1,0:T(8,128)S(1)} %collective-permute-done.12.refs_2_, f32[8,32,128]{2,1,0:T(8,128)S(1)} %collective-permute-done.13.refs_3_), custom_call_target="tpu_custom_call" | custom-call | tf_op jit(solution)/shard_map/scale/pallas_call | solution.py:353
  (8 shorter events, 0.1 us)
Async XLA Ops:
  0.0 9.2 %copy-start.1 = (s32[1,128,256]{2,1,0:T(8,128)S(1)}, s32[1,128,256]{2,1,0:T(8,128)}, u32[]{:S(2)}) copy-start(s32[1,128,256]{2,1,0:T(8,128)} %samples.3) | copy-start | bytes 393220
  0.0 9.2 %copy-start = (bf16[320,16384]{1,0:T(8,128)(2,1)S(1)}, bf16[320,16384]{1,0:T(8,128)(2,1)}, u32[]{:S(2)}) copy-start(bf16[320,16384]{1,0:T(8,128)(2,1)} %matrix.3) | copy-start | bytes 31457284
  6.8 2.4 %collective-permute-start = (f32[2,8,96,128]{3,2,1,0:T(8,128)S(1)}, f32[2,8,96,128]{3,2,1,0:T(8,128)S(1)}, u32[]{:S(2)}, u32[]{:S(2)}) collective-permute-start(f32[2,8,96,128]{3,2,1,0:T(8,128)S(1)} %get-tuple-element.25), channel_id=1, source_target_pairs={{0,1},{1,0},{2,3},{3,2},{4,5},{5,4},{6,7},{7,6},{8,9},{9,8},{10,11... | collective-permute-start | bytes 2359304 | tf_op jit(solution)/shard_map/ppermute | solution.py:229
  15.3 2.8 %collective-permute-start.2 = (f32[2,8,48,128]{3,2,1,0:T(8,128)S(1)}, f32[2,8,48,128]{3,2,1,0:T(8,128)S(1)}, u32[]{:S(2)}, u32[]{:S(2)}) collective-permute-start(f32[2,8,48,128]{3,2,1,0:T(8,128)S(1)} %get-tuple-element.28), channel_id=1, source_target_pairs={{0,1},{1,0},{2,3},{3,2},{4,5},{5,4},{6,7},{7,6},{8,9},{9,8},{10,11... | collective-permute-start | bytes 1179656 | tf_op jit(solution)/shard_map/ppermute | solution.py:229
  15.5 12.0 %collective-permute-start.1 = (f32[8,96,128]{2,1,0:T(8,128)S(1)}, f32[8,96,128]{2,1,0:T(8,128)S(1)}, u32[]{:S(2)}, u32[]{:S(2)}) collective-permute-start(f32[8,96,128]{2,1,0:T(8,128)S(1)} %fusion.after), channel_id=1, source_target_pairs={{0,2},{1,3},{2,0},{3,1},{4,6},{5,7},{6,4},{7,5},{8,10},{9,11},{10,... | collective-permute-start | bytes 1179656 | tf_op jit(solution)/shard_map/ppermute | solution.py:229
  18.1 13.5 %collective-permute-start.3 = (f32[8,48,128]{2,1,0:T(8,128)S(1)}, f32[8,48,128]{2,1,0:T(8,128)S(1)}, u32[]{:S(2)}, u32[]{:S(2)}) collective-permute-start(f32[8,48,128]{2,1,0:T(8,128)S(1)} %fusion.1), channel_id=1, source_target_pairs={{0,2},{1,3},{2,0},{3,1},{4,6},{5,7},{6,4},{7,5},{8,10},{9,11},{10,... | collective-permute-start | bytes 589832 | tf_op jit(solution)/shard_map/ppermute | solution.py:229
  31.7 5.7 %collective-permute-start.4 = (f32[144,128]{1,0:T(8,128)S(1)}, f32[144,128]{1,0:T(8,128)S(1)}, u32[]{:S(2)}, u32[]{:S(2)}) collective-permute-start(f32[144,128]{1,0:T(8,128)S(1)} %get-tuple-element.31), channel_id=1, source_target_pairs={{0,4},{4,0},{8,12},{12,8},{16,20},{20,16},{24,28},{28,24},{1,5},{5... | collective-permute-start | bytes 221192 | tf_op jit(solution)/shard_map/ppermute | solution.py:229
  31.8 9.2 %collective-permute-start.5 = (f32[144,128]{1,0:T(8,128)S(1)}, f32[144,128]{1,0:T(8,128)S(1)}, u32[]{:S(2)}, u32[]{:S(2)}) collective-permute-start(f32[144,128]{1,0:T(8,128)S(1)} %get-tuple-element.32), channel_id=1, source_target_pairs={{0,8},{4,12},{8,0},{12,4},{16,24},{20,28},{24,16},{28,20},{1,9},{5... | collective-permute-start | bytes 221192 | tf_op jit(solution)/shard_map/ppermute | solution.py:229
  33.6 7.4 %collective-permute-start.6 = (f32[144,128]{1,0:T(8,128)S(1)}, f32[144,128]{1,0:T(8,128)S(1)}, u32[]{:S(2)}, u32[]{:S(2)}) collective-permute-start(f32[144,128]{1,0:T(8,128)S(1)} %get-tuple-element.33), channel_id=1, source_target_pairs={{0,12},{4,8},{8,4},{12,0},{16,28},{20,24},{24,20},{28,16},{1,13},{... | collective-permute-start | bytes 221192 | tf_op jit(solution)/shard_map/ppermute | solution.py:229
  34.5 6.6 %collective-permute-start.7 = (f32[144,128]{1,0:T(8,128)S(1)}, f32[144,128]{1,0:T(8,128)S(1)}, u32[]{:S(2)}, u32[]{:S(2)}) collective-permute-start(f32[144,128]{1,0:T(8,128)S(1)} %get-tuple-element.34), channel_id=1, source_target_pairs={{0,16},{4,20},{8,24},{12,28},{16,0},{20,4},{24,8},{28,12},{1,17},{... | collective-permute-start | bytes 221192 | tf_op jit(solution)/shard_map/ppermute | solution.py:229
  36.6 11.1 %collective-permute-start.8 = (f32[144,128]{1,0:T(8,128)S(1)}, f32[144,128]{1,0:T(8,128)S(1)}, u32[]{:S(2)}, u32[]{:S(2)}) collective-permute-start(f32[144,128]{1,0:T(8,128)S(1)} %get-tuple-element.35), channel_id=1, source_target_pairs={{0,20},{4,16},{8,28},{12,24},{16,4},{20,0},{24,12},{28,8},{1,21},{... | collective-permute-start | bytes 221192 | tf_op jit(solution)/shard_map/ppermute | solution.py:229
  37.5 10.2 %collective-permute-start.9 = (f32[144,128]{1,0:T(8,128)S(1)}, f32[144,128]{1,0:T(8,128)S(1)}, u32[]{:S(2)}, u32[]{:S(2)}) collective-permute-start(f32[144,128]{1,0:T(8,128)S(1)} %get-tuple-element.36), channel_id=1, source_target_pairs={{0,24},{4,28},{8,16},{12,20},{16,8},{20,12},{24,0},{28,4},{1,25},{... | collective-permute-start | bytes 221192 | tf_op jit(solution)/shard_map/ppermute | solution.py:229
  41.0 6.6 %collective-permute-start.10 = (f32[144,128]{1,0:T(8,128)S(1)}, f32[144,128]{1,0:T(8,128)S(1)}, u32[]{:S(2)}, u32[]{:S(2)}) collective-permute-start(f32[144,128]{1,0:T(8,128)S(1)} %get-tuple-element.37), channel_id=1, source_target_pairs={{0,28},{4,24},{8,20},{12,16},{16,12},{20,8},{24,4},{28,0},{1,29},{... | collective-permute-start | bytes 221192 | tf_op jit(solution)/shard_map/ppermute | solution.py:229
  48.8 5.2 %collective-permute-start.11 = (f32[8,32,128]{2,1,0:T(8,128)S(1)}, f32[8,32,128]{2,1,0:T(8,128)S(1)}, u32[]{:S(2)}, u32[]{:S(2)}) collective-permute-start(f32[8,32,128]{2,1,0:T(8,128)S(1)} %get-tuple-element.40), channel_id=1, source_target_pairs={{0,1},{1,0},{2,3},{3,2},{4,5},{5,4},{6,7},{7,6},{8,9},{9,8},{10,11... | collective-permute-start | bytes 393224 | tf_op jit(solution)/shard_map/ppermute | solution.py:229
  52.1 5.0 %collective-permute-start.12 = (f32[8,32,128]{2,1,0:T(8,128)S(1)}, f32[8,32,128]{2,1,0:T(8,128)S(1)}, u32[]{:S(2)}, u32[]{:S(2)}) collective-permute-start(f32[8,32,128]{2,1,0:T(8,128)S(1)} %get-tuple-element.41), channel_id=1, source_target_pairs={{0,2},{1,3},{2,0},{3,1},{4,6},{5,7},{6,4},{7,5},{8,10},{9,11},{10,... | collective-permute-start | bytes 393224 | tf_op jit(solution)/shard_map/ppermute | solution.py:229
  53.3 6.8 %collective-permute-start.13 = (f32[8,32,128]{2,1,0:T(8,128)S(1)}, f32[8,32,128]{2,1,0:T(8,128)S(1)}, u32[]{:S(2)}, u32[]{:S(2)}) collective-permute-start(f32[8,32,128]{2,1,0:T(8,128)S(1)} %get-tuple-element.42), channel_id=1, source_target_pairs={{0,3},{1,2},{2,1},{3,0},{4,7},{5,6},{6,5},{7,4},{8,11},{9,10},{10,... | collective-permute-start | bytes 393224 | tf_op jit(solution)/shard_map/ppermute | solution.py:229

commit v2 on v1

--- a/solution.py
+++ b/solution.py
@@ -28,33 +28,41 @@
         self.rows_total = self.rows_dev * self.rows_axis * self.grp_axis
 
 
-def list_live(n, first, last, live, counts):
+def list_live(n, first, last, live, lists, counts, pairs, each=None):
     me = lax.axis_index("rows")
 
     def scan(o, found):
         r = jnp.bitwise_xor(o, me)
         top = jnp.minimum(counts[me, r], last)
-
-        def add(k, found):
-            live[found] = o * n.cap + k
-            return found + 1
-
-        return lax.fori_loop(first, top, add, found)
+        for k in range(first, last):
+
+            @pl.when(k < top)
+            def _(k=k):
+                at = found + (k - first)
+                pair = lists[me, k, r]
+                live[0, at] = o * n.cap + k
+                live[1, at] = pairs[0, pair]
+                live[2, at] = pairs[1, pair]
+                if each is not None:
+                    each(at, pairs[0, pair], pairs[1, pair])
+
+        return found + jnp.maximum(top - first, 0)
 
     return lax.fori_loop(0, n.rows_axis, scan, 0)
 
 
-def multiply(n, first, slots, loads, samples, blocks_of, stage, outs):
+def multiply(n, first, at, live, loads, samples, stage, outs):
     g = lax.axis_index("grp")
     positions = lax.broadcasted_iota(jnp.int32, (n.rows_dev, n.samples), 0)
-    for u, t in enumerate(slots):
-        drawn = samples[pl.ds(blocks_of(t)[0], 1), :]
+    for u in range(unroll):
+        drawn = samples[pl.ds(live[1, at[u]], 1), :]
         times = jnp.sum(jnp.where(drawn == positions, 1.0, 0.0), axis=1, keepdims=True)
-        left, right = loads(u, t)
+        left, right = loads(at[u])
         weighted = (times * left.astype(jnp.float32)).astype(jnp.bfloat16)
         stage[u] = lax.dot_general(
             weighted, right, (((0,), (0,)), ((), ())), preferred_element_type=jnp.float32
         )
+    slots = [live[0, a] for a in at]
     for u, t in enumerate(slots):
         o = t // n.cap
         row = pl.multiple_of((t % n.cap - first) * n.part, n.part)
@@ -81,50 +89,37 @@
 def early_kernel(n, last, lists, counts, pairs, samples, matrix, *rest):
     outs = split_outs(n, rest[: 1 + n.grp_axis // 2])
     held, drawn, stage, live, arrive, came = rest[1 + n.grp_axis // 2 :]
-    me = lax.axis_index("rows")
     draws = pltpu.make_async_copy(samples.at[0], drawn, came)
     draws.start()
 
-    def blocks_of(t):
-        pair = lists[me, t % n.cap, jnp.bitwise_xor(t // n.cap, me)]
-        return pairs[0, pair], pairs[1, pair]
-
-    def copies(i, t):
-        both = blocks_of(t)
+    def copies(i, b, c):
         return [
             pltpu.make_async_copy(
-                matrix.at[:, pl.ds(pl.multiple_of(both[side] * n.width, n.width), n.width)],
+                matrix.at[:, pl.ds(pl.multiple_of(block * n.width, n.width), n.width)],
                 held.at[i, side],
                 arrive.at[i],
             )
-            for side in range(2)
+            for side, block in enumerate((b, c))
         ]
 
-    found = list_live(n, 0, last, live, counts)
-
-    def begin(i, carry):
-        for copy in copies(i, live[i]):
+    def begin(i, b, c):
+        for copy in copies(i, b, c):
             copy.start()
-        return carry
-
-    lax.fori_loop(0, found, begin, 0)
+
+    found = list_live(n, 0, last, live, lists, counts, pairs, begin)
     clear(outs, n, last * n.part)
     draws.wait()
 
     def group(i, carry):
         at = [jnp.where(i * unroll + u < found, i * unroll + u, 0) for u in range(unroll)]
-        slots = [live[a] for a in at]
         for u in range(unroll):
 
             @pl.when(i * unroll + u < found)
             def _(u=u):
-                for copy in copies(at[u], slots[u]):
+                for copy in copies(at[u], live[1, at[u]], live[2, at[u]]):
                     copy.wait()
 
-        def loads(u, t):
-            return held[at[u], 0], held[at[u], 1]
-
-        multiply(n, 0, slots, loads, drawn, blocks_of, stage, outs)
+        multiply(n, 0, at, live, lambda a: (held[a, 0], held[a, 1]), drawn, stage, outs)
         return carry
 
     lax.fori_loop(0, pl.cdiv(found, unroll), group, 0)
@@ -136,7 +131,7 @@
     me = lax.axis_index("rows")
     g = lax.axis_index("grp")
     tile_rows = (n.cap - first) * n.part
-    found = list_live(n, first, n.cap, live, counts)
+    found = list_live(n, first, n.cap, live, lists, counts, pairs)
     clear(outs, n, tile_rows)
 
     def columns(b):
@@ -147,7 +142,7 @@
         sums[pl.ds(b, 1), :] = jnp.sum(x * x, axis=0, keepdims=True)
         return carry
 
-    lax.fori_loop(0, n.blocks, block_sum, 0, unroll=4)
+    lax.fori_loop(0, n.blocks, block_sum, 0, unroll=8)
 
     for d in range(n.grp_axis):
 
@@ -161,18 +156,13 @@
 
         lax.fori_loop(0, n.rows_axis, place, 0)
 
-    def blocks_of(t):
-        pair = lists[me, t % n.cap, jnp.bitwise_xor(t // n.cap, me)]
-        return pairs[0, pair], pairs[1, pair]
-
     def group(i, carry):
-        slots = [live[jnp.where(i * unroll + u < found, i * unroll + u, 0)] for u in range(unroll)]
-
-        def loads(u, t):
-            both = blocks_of(t)
-            return columns(both[0]), columns(both[1])
-
-        multiply(n, first, slots, loads, samples.at[0], blocks_of, stage, outs)
+        at = [jnp.where(i * unroll + u < found, i * unroll + u, 0) for u in range(unroll)]
+
+        def loads(a):
+            return columns(live[1, a]), columns(live[2, a])
+
+        multiply(n, first, at, live, loads, samples.at[0], stage, outs)
         return carry
 
     lax.fori_loop(0, pl.cdiv(found, unroll), group, 0)
@@ -263,7 +253,7 @@
             pltpu.VMEM((slots, 2, n.rows_dev, n.width), matrix.dtype),
             pltpu.VMEM(sample_rows.shape[1:], jnp.int32),
             pltpu.VMEM(stage, f32),
-            pltpu.SMEM((slots,), jnp.int32),
+            pltpu.SMEM((3, slots), jnp.int32),
             pltpu.SemaphoreType.DMA((slots,)),
             pltpu.SemaphoreType.DMA,
         ],
@@ -300,7 +290,7 @@
         scratch_shapes=[
             pltpu.VMEM((n.blocks, n.width), f32),
             pltpu.VMEM(stage, f32),
-            pltpu.SMEM((slots,), jnp.int32),
+            pltpu.SMEM((3, slots), jnp.int32),
         ],
         compiler_params=megabytes(
             stage, (n.blocks, n.width), sample_rows.shape, (n.grp_axis, n.rows_axis, late_rows, n.width)
@@ -337,10 +327,10 @@
         scratch_shapes=[pltpu.VMEM((n.region, n.part, n.width), f32)],
         compiler_params=megabytes((n.rows_axis,) + message, (2 * n.grp_axis,) + quarter),
         name="gather",
-    )(lists, *came)
-    came = [owned[0]] + [
-        swap(owned[d], "grp", n.grp_axis, d) for d in reversed(range(1, n.grp_axis))
-    ][::-1]
+    )(jnp.transpose(pair_list, (0, 2, 1)), *came)
+    came = [owned[0]]
+    for d in range(1, n.grp_axis):
+        came.append(swap(owned[d], "grp", n.grp_axis, d))
     tiles = (n.own, n.width, n.width)
     factor = pl.pallas_call(
         functools.partial(factor_kernel, n),

time: 61.4 us -> 60.8 us (level)
  no operation moved by 1% of the time
where the time goes in v2:
time: 60.8 us; the launch traced here: 60.4 us
  waiting for transfers between devices  27.1 us (45%)
  starting transfers between devices  18.5 us (30%)
  Pallas kernels  14.6 us (24%)
    ppermute x14, waiting for transfers between devices, swap(): return lax.ppermute(x, axis, [(i, i ^ distance) for i in range(size)])  27.1 us
    ppermute x14, starting transfers between devices, swap(): return lax.ppermute(x, axis, [(i, i ^ distance) for i in range(size)])  18.5 us
    pallas_call x1, Pallas kernels, shards(): pl.pallas_call(functools.partial(early_kernel, n, first), out_shape=stage...  6.71 us
    pallas_call x1, Pallas kernels, shards(): pl.pallas_call(functools.partial(late_kernel, n, first), out_shape=stage_...  5.74 us
  transfers between devices with their start and end apart: 14, of which 6 were waited for; matrix products, arithmetic and copies ran while one was open for 0% of the time, Pallas kernels for 0%

profile of v2, /device:TPU:1, one launch (start us, length us, event | category | flops | bytes accessed | tf_op | source)
XLA Modules:
  0.0 60.4 jit_solution(7312916648117094518)
XLA Ops:
  0.0 6.7 %early_tiles.1 = (f32[2,8,96,128]{3,2,1,0:T(8,128)S(1)}, f32[8,96,128]{2,1,0:T(8,128)S(1)}, f32[8,96,128]{2,1,0:T(8,128)S(1)}) custom-call(s32[8,4,8]{2,1,0:T(4,128)} %bitcast.10, s32[8,8]{1,0:T(8,128)} %counts.3, s32[2,256]{1,0:T(2,128)} %bitcast.13, s32[1,128,256]{2,1,0:T(8,128)} %samples.3, bf16[320,16384]{1,0:T(8,128)(2,1)} %matrix.3), custom_call_target="tpu_custom_call" | custom-call | tf_op jit(solution)/shard_map/early_tiles/pallas_call | solution.py:247
  6.7 0.1 collective-permute-start
  6.8 2.3 %collective-permute-done.refs_1_ = f32[2,8,96,128]{3,2,1,0:T(8,128)S(1)} collective-permute-done((f32[2,8,96,128]{3,2,1,0:T(8,128)S(1)}, f32[2,8,96,128]{3,2,1,0:T(8,128)S(1)}, u32[]{:S(2)}, u32[]{:S(2)}) %collective-permute-start) | collective-permute-done | bytes 786464 | tf_op jit(solution)/shard_map/ppermute | solution.py:219
  9.1 5.7 %late_tiles.1 = (f32[2,8,48,128]{3,2,1,0:T(8,128)S(1)}, f32[8,48,128]{2,1,0:T(8,128)S(1)}, f32[8,48,128]{2,1,0:T(8,128)S(1)}) custom-call(s32[8,4,8]{2,1,0:T(4,128)} %bitcast.11, s32[8,8]{1,0:T(8,128)} %counts.3, s32[2,256]{1,0:T(2,128)} %bitcast.14, s32[1,128,256]{2,1,0:T(8,128)S(1)} %copy-done.1, bf16[320,16384]{1,0:T(8,128)(2,1)S(1)} %copy-done, ...), custom_call_target="tpu_custom_call" | custom-call | flops 267386880 | bytes 10485760 | tf_op jit(solution)/shard_map/late_tiles/pallas_call | solution.py:285
  14.9 0.2 collective-permute-start.2
  15.1 2.6 %collective-permute-start.1 = (f32[8,96,128]{2,1,0:T(8,128)S(1)}, f32[8,96,128]{2,1,0:T(8,128)S(1)}, u32[]{:S(2)}, u32[]{:S(2)}) collective-permute-start(f32[8,96,128]{2,1,0:T(8,128)S(1)} %fusion.after), channel_id=1, source_target_pairs={{0,2},{1,3},{2,0},{3,1},{4,6},{5,7},{6,4},{7,5},{8,10},{9,11},{10,... | collective-permute-start | bytes 1179656 | tf_op jit(solution)/shard_map/ppermute | solution.py:219
  17.7 0.0 collective-permute-done.2.refs_4_
  17.7 1.4 %collective-permute-start.3 = (f32[8,48,128]{2,1,0:T(8,128)S(1)}, f32[8,48,128]{2,1,0:T(8,128)S(1)}, u32[]{:S(2)}, u32[]{:S(2)}) collective-permute-start(f32[8,48,128]{2,1,0:T(8,128)S(1)} %fusion.1), channel_id=1, source_target_pairs={{0,2},{1,3},{2,0},{3,1},{4,6},{5,7},{6,4},{7,5},{8,10},{9,11},{10,... | collective-permute-start | bytes 589832 | tf_op jit(solution)/shard_map/ppermute | solution.py:219
  19.1 7.9 %collective-permute-done.1.refs_2_ = f32[8,96,128]{2,1,0:T(8,128)S(1)} collective-permute-done((f32[8,96,128]{2,1,0:T(8,128)S(1)}, f32[8,96,128]{2,1,0:T(8,128)S(1)}, u32[]{:S(2)}, u32[]{:S(2)}) %collective-permute-start.1) | collective-permute-done | bytes 393248 | tf_op jit(solution)/shard_map/ppermute | solution.py:219
  27.0 4.2 %collective-permute-done.3.refs_5_ = f32[8,48,128]{2,1,0:T(8,128)S(1)} collective-permute-done((f32[8,48,128]{2,1,0:T(8,128)S(1)}, f32[8,48,128]{2,1,0:T(8,128)S(1)}, u32[]{:S(2)}, u32[]{:S(2)}) %collective-permute-start.3) | collective-permute-done | bytes 196640 | tf_op jit(solution)/shard_map/ppermute | solution.py:219
  31.3 0.1 spread.1
  31.4 0.1 collective-permute-start.4
  31.4 1.8 %collective-permute-start.5 = (f32[144,128]{1,0:T(8,128)S(1)}, f32[144,128]{1,0:T(8,128)S(1)}, u32[]{:S(2)}, u32[]{:S(2)}) collective-permute-start(f32[144,128]{1,0:T(8,128)S(1)} %get-tuple-element.32), channel_id=1, source_target_pairs={{0,8},{4,12},{8,0},{12,4},{16,24},{20,28},{24,16},{28,20},{1,9},{5... | collective-permute-start | bytes 221192 | tf_op jit(solution)/shard_map/ppermute | solution.py:219
  33.3 0.8 %collective-permute-start.6 = (f32[144,128]{1,0:T(8,128)S(1)}, f32[144,128]{1,0:T(8,128)S(1)}, u32[]{:S(2)}, u32[]{:S(2)}) collective-permute-start(f32[144,128]{1,0:T(8,128)S(1)} %get-tuple-element.33), channel_id=1, source_target_pairs={{0,12},{4,8},{8,4},{12,0},{16,28},{20,24},{24,20},{28,16},{1,13},{... | collective-permute-start | bytes 221192 | tf_op jit(solution)/shard_map/ppermute | solution.py:219
  34.1 2.1 %collective-permute-start.7 = (f32[144,128]{1,0:T(8,128)S(1)}, f32[144,128]{1,0:T(8,128)S(1)}, u32[]{:S(2)}, u32[]{:S(2)}) collective-permute-start(f32[144,128]{1,0:T(8,128)S(1)} %get-tuple-element.34), channel_id=1, source_target_pairs={{0,16},{4,20},{8,24},{12,28},{16,0},{20,4},{24,8},{28,12},{1,17},{... | collective-permute-start | bytes 221192 | tf_op jit(solution)/shard_map/ppermute | solution.py:219
  36.2 0.9 %collective-permute-start.8 = (f32[144,128]{1,0:T(8,128)S(1)}, f32[144,128]{1,0:T(8,128)S(1)}, u32[]{:S(2)}, u32[]{:S(2)}) collective-permute-start(f32[144,128]{1,0:T(8,128)S(1)} %get-tuple-element.35), channel_id=1, source_target_pairs={{0,20},{4,16},{8,28},{12,24},{16,4},{20,0},{24,12},{28,8},{1,21},{... | collective-permute-start | bytes 221192 | tf_op jit(solution)/shard_map/ppermute | solution.py:219
  37.1 0.0 collective-permute-done.4.refs_1_
  37.1 3.5 %collective-permute-start.9 = (f32[144,128]{1,0:T(8,128)S(1)}, f32[144,128]{1,0:T(8,128)S(1)}, u32[]{:S(2)}, u32[]{:S(2)}) collective-permute-start(f32[144,128]{1,0:T(8,128)S(1)} %get-tuple-element.36), channel_id=1, source_target_pairs={{0,24},{4,28},{8,16},{12,20},{16,8},{20,12},{24,0},{28,4},{1,25},{... | collective-permute-start | bytes 221192 | tf_op jit(solution)/shard_map/ppermute | solution.py:219
  40.6 0.0 collective-permute-done.5.refs_2_
  40.6 0.0 collective-permute-start.10
  40.6 0.0 collective-permute-done.6.refs_3_
  40.7 6.6 %collective-permute-done.8.refs_5_ = f32[144,128]{1,0:T(8,128)S(1)} collective-permute-done((f32[144,128]{1,0:T(8,128)S(1)}, f32[144,128]{1,0:T(8,128)S(1)}, u32[]{:S(2)}, u32[]{:S(2)}) %collective-permute-start.8) | collective-permute-done | bytes 73760 | tf_op jit(solution)/shard_map/ppermute | solution.py:219
  47.3 0.0 collective-permute-done.9.refs_6_
  47.3 0.0 collective-permute-done.10.refs_7_
  47.3 1.0 %gather.1 = (f32[8,32,128]{2,1,0:T(8,128)S(1)}, f32[8,32,128]{2,1,0:T(8,128)S(1)}, f32[8,32,128]{2,1,0:T(8,128)S(1)}, f32[8,32,128]{2,1,0:T(8,128)S(1)}, f32[16,128]{1,0:T(8,128)S(1)}) custom-call(s32[8,4,8]{2,1,0:T(4,128)S(1)} %bitcast.12, f32[144,128]{1,0:T(8,128)S(1)} %get-tuple-element.30.refs_0_, f32[144,128]{1,0:T(8,128)S(1)} %collective-permute-done.4.refs_1_, ...), custom_call_target="tpu_custom_call" | custom-call | tf_op jit(solution)/shard_map/gather/pallas_call | solution.py:321
  48.3 3.2 %collective-permute-start.11 = (f32[8,32,128]{2,1,0:T(8,128)S(1)}, f32[8,32,128]{2,1,0:T(8,128)S(1)}, u32[]{:S(2)}, u32[]{:S(2)}) collective-permute-start(f32[8,32,128]{2,1,0:T(8,128)S(1)} %get-tuple-element.40), channel_id=1, source_target_pairs={{0,1},{1,0},{2,3},{3,2},{4,5},{5,4},{6,7},{7,6},{8,9},{9,8},{10,11... | collective-permute-start | bytes 393224 | tf_op jit(solution)/shard_map/ppermute | solution.py:219
  51.6 1.2 %collective-permute-start.12 = (f32[8,32,128]{2,1,0:T(8,128)S(1)}, f32[8,32,128]{2,1,0:T(8,128)S(1)}, u32[]{:S(2)}, u32[]{:S(2)}) collective-permute-start(f32[8,32,128]{2,1,0:T(8,128)S(1)} %get-tuple-element.41), channel_id=1, source_target_pairs={{0,2},{1,3},{2,0},{3,1},{4,6},{5,7},{6,4},{7,5},{8,10},{9,11},{10,... | collective-permute-start | bytes 393224 | tf_op jit(solution)/shard_map/ppermute | solution.py:219
  52.8 0.5 collective-permute-start.13
  53.3 0.2 factor.1
  53.5 3.0 %collective-permute-done.12.refs_2_ = f32[8,32,128]{2,1,0:T(8,128)S(1)} collective-permute-done((f32[8,32,128]{2,1,0:T(8,128)S(1)}, f32[8,32,128]{2,1,0:T(8,128)S(1)}, u32[]{:S(2)}, u32[]{:S(2)}) %collective-permute-start.12) | collective-permute-done | bytes 131104 | tf_op jit(solution)/shard_map/ppermute | solution.py:219
  56.5 3.1 %collective-permute-done.13.refs_3_ = f32[8,32,128]{2,1,0:T(8,128)S(1)} collective-permute-done((f32[8,32,128]{2,1,0:T(8,128)S(1)}, f32[8,32,128]{2,1,0:T(8,128)S(1)}, u32[]{:S(2)}, u32[]{:S(2)}) %collective-permute-start.13) | collective-permute-done | bytes 131104 | tf_op jit(solution)/shard_map/ppermute | solution.py:219
  59.6 0.8 %scale.1 = f32[8,128,128]{2,1,0:T(8,128)} custom-call(f32[8,128,128]{2,1,0:T(8,128)S(1)} %factor.1, f32[8,32,128]{2,1,0:T(8,128)S(1)} %get-tuple-element.39.refs_0_, f32[8,32,128]{2,1,0:T(8,128)S(1)} %collective-permute-done.11.refs_1_, f32[8,32,128]{2,1,0:T(8,128)S(1)} %collective-permute-done.12.refs_2_, f32[8,32,128]{2,1,0:T(8,128)S(1)} %collective-permute-done.13.refs_3_), custom_call_target="tpu_custom_call" | custom-call | tf_op jit(solution)/shard_map/scale/pallas_call | solution.py:343
  (10 shorter events, 0.1 us)
Async XLA Ops:
  0.0 9.1 %copy-start.1 = (s32[1,128,256]{2,1,0:T(8,128)S(1)}, s32[1,128,256]{2,1,0:T(8,128)}, u32[]{:S(2)}) copy-start(s32[1,128,256]{2,1,0:T(8,128)} %samples.3) | copy-start | bytes 393220
  0.0 9.1 %copy-start = (bf16[320,16384]{1,0:T(8,128)(2,1)S(1)}, bf16[320,16384]{1,0:T(8,128)(2,1)}, u32[]{:S(2)}) copy-start(bf16[320,16384]{1,0:T(8,128)(2,1)} %matrix.3) | copy-start | bytes 31457284
  0.0 47.3 %copy-start.2 = (s32[8,8,4]{1,2,0:T(4,128)S(1)}, s32[8,8,4]{1,2,0:T(4,128)}, u32[]{:S(2)}) copy-start(s32[8,8,4]{1,2,0:T(4,128)} %param.7) | copy-start | bytes 3076
  6.7 2.4 %collective-permute-start = (f32[2,8,96,128]{3,2,1,0:T(8,128)S(1)}, f32[2,8,96,128]{3,2,1,0:T(8,128)S(1)}, u32[]{:S(2)}, u32[]{:S(2)}) collective-permute-start(f32[2,8,96,128]{3,2,1,0:T(8,128)S(1)} %get-tuple-element.25), channel_id=1, source_target_pairs={{0,1},{1,0},{2,3},{3,2},{4,5},{5,4},{6,7},{7,6},{8,9},{9,8},{10,11... | collective-permute-start | bytes 2359304 | tf_op jit(solution)/shard_map/ppermute | solution.py:219
  14.9 2.8 %collective-permute-start.2 = (f32[2,8,48,128]{3,2,1,0:T(8,128)S(1)}, f32[2,8,48,128]{3,2,1,0:T(8,128)S(1)}, u32[]{:S(2)}, u32[]{:S(2)}) collective-permute-start(f32[2,8,48,128]{3,2,1,0:T(8,128)S(1)} %get-tuple-element.28), channel_id=1, source_target_pairs={{0,1},{1,0},{2,3},{3,2},{4,5},{5,4},{6,7},{7,6},{8,9},{9,8},{10,11... | collective-permute-start | bytes 1179656 | tf_op jit(solution)/shard_map/ppermute | solution.py:219
  15.1 11.9 %collective-permute-start.1 = (f32[8,96,128]{2,1,0:T(8,128)S(1)}, f32[8,96,128]{2,1,0:T(8,128)S(1)}, u32[]{:S(2)}, u32[]{:S(2)}) collective-permute-start(f32[8,96,128]{2,1,0:T(8,128)S(1)} %fusion.after), channel_id=1, source_target_pairs={{0,2},{1,3},{2,0},{3,1},{4,6},{5,7},{6,4},{7,5},{8,10},{9,11},{10,... | collective-permute-start | bytes 1179656 | tf_op jit(solution)/shard_map/ppermute | solution.py:219
  17.7 13.5 %collective-permute-start.3 = (f32[8,48,128]{2,1,0:T(8,128)S(1)}, f32[8,48,128]{2,1,0:T(8,128)S(1)}, u32[]{:S(2)}, u32[]{:S(2)}) collective-permute-start(f32[8,48,128]{2,1,0:T(8,128)S(1)} %fusion.1), channel_id=1, source_target_pairs={{0,2},{1,3},{2,0},{3,1},{4,6},{5,7},{6,4},{7,5},{8,10},{9,11},{10,... | collective-permute-start | bytes 589832 | tf_op jit(solution)/shard_map/ppermute | solution.py:219
  31.4 5.7 %collective-permute-start.4 = (f32[144,128]{1,0:T(8,128)S(1)}, f32[144,128]{1,0:T(8,128)S(1)}, u32[]{:S(2)}, u32[]{:S(2)}) collective-permute-start(f32[144,128]{1,0:T(8,128)S(1)} %get-tuple-element.31), channel_id=1, source_target_pairs={{0,4},{4,0},{8,12},{12,8},{16,20},{20,16},{24,28},{28,24},{1,5},{5... | collective-permute-start | bytes 221192 | tf_op jit(solution)/shard_map/ppermute | solution.py:219
  31.4 9.2 %collective-permute-start.5 = (f32[144,128]{1,0:T(8,128)S(1)}, f32[144,128]{1,0:T(8,128)S(1)}, u32[]{:S(2)}, u32[]{:S(2)}) collective-permute-start(f32[144,128]{1,0:T(8,128)S(1)} %get-tuple-element.32), channel_id=1, source_target_pairs={{0,8},{4,12},{8,0},{12,4},{16,24},{20,28},{24,16},{28,20},{1,9},{5... | collective-permute-start | bytes 221192 | tf_op jit(solution)/shard_map/ppermute | solution.py:219
  33.3 7.4 %collective-permute-start.6 = (f32[144,128]{1,0:T(8,128)S(1)}, f32[144,128]{1,0:T(8,128)S(1)}, u32[]{:S(2)}, u32[]{:S(2)}) collective-permute-start(f32[144,128]{1,0:T(8,128)S(1)} %get-tuple-element.33), channel_id=1, source_target_pairs={{0,12},{4,8},{8,4},{12,0},{16,28},{20,24},{24,20},{28,16},{1,13},{... | collective-permute-start | bytes 221192 | tf_op jit(solution)/shard_map/ppermute | solution.py:219
  34.1 6.6 %collective-permute-start.7 = (f32[144,128]{1,0:T(8,128)S(1)}, f32[144,128]{1,0:T(8,128)S(1)}, u32[]{:S(2)}, u32[]{:S(2)}) collective-permute-start(f32[144,128]{1,0:T(8,128)S(1)} %get-tuple-element.34), channel_id=1, source_target_pairs={{0,16},{4,20},{8,24},{12,28},{16,0},{20,4},{24,8},{28,12},{1,17},{... | collective-permute-start | bytes 221192 | tf_op jit(solution)/shard_map/ppermute | solution.py:219
  36.2 11.1 %collective-permute-start.8 = (f32[144,128]{1,0:T(8,128)S(1)}, f32[144,128]{1,0:T(8,128)S(1)}, u32[]{:S(2)}, u32[]{:S(2)}) collective-permute-start(f32[144,128]{1,0:T(8,128)S(1)} %get-tuple-element.35), channel_id=1, source_target_pairs={{0,20},{4,16},{8,28},{12,24},{16,4},{20,0},{24,12},{28,8},{1,21},{... | collective-permute-start | bytes 221192 | tf_op jit(solution)/shard_map/ppermute | solution.py:219
  37.1 10.2 %collective-permute-start.9 = (f32[144,128]{1,0:T(8,128)S(1)}, f32[144,128]{1,0:T(8,128)S(1)}, u32[]{:S(2)}, u32[]{:S(2)}) collective-permute-start(f32[144,128]{1,0:T(8,128)S(1)} %get-tuple-element.36), channel_id=1, source_target_pairs={{0,24},{4,28},{8,16},{12,20},{16,8},{20,12},{24,0},{28,4},{1,25},{... | collective-permute-start | bytes 221192 | tf_op jit(solution)/shard_map/ppermute | solution.py:219
  40.6 6.6 %collective-permute-start.10 = (f32[144,128]{1,0:T(8,128)S(1)}, f32[144,128]{1,0:T(8,128)S(1)}, u32[]{:S(2)}, u32[]{:S(2)}) collective-permute-start(f32[144,128]{1,0:T(8,128)S(1)} %get-tuple-element.37), channel_id=1, source_target_pairs={{0,28},{4,24},{8,20},{12,16},{16,12},{20,8},{24,4},{28,0},{1,29},{... | collective-permute-start | bytes 221192 | tf_op jit(solution)/shard_map/ppermute | solution.py:219
  48.3 5.2 %collective-permute-start.11 = (f32[8,32,128]{2,1,0:T(8,128)S(1)}, f32[8,32,128]{2,1,0:T(8,128)S(1)}, u32[]{:S(2)}, u32[]{:S(2)}) collective-permute-start(f32[8,32,128]{2,1,0:T(8,128)S(1)} %get-tuple-element.40), channel_id=1, source_target_pairs={{0,1},{1,0},{2,3},{3,2},{4,5},{5,4},{6,7},{7,6},{8,9},{9,8},{10,11... | collective-permute-start | bytes 393224 | tf_op jit(solution)/shard_map/ppermute | solution.py:219
  51.6 5.0 %collective-permute-start.12 = (f32[8,32,128]{2,1,0:T(8,128)S(1)}, f32[8,32,128]{2,1,0:T(8,128)S(1)}, u32[]{:S(2)}, u32[]{:S(2)}) collective-permute-start(f32[8,32,128]{2,1,0:T(8,128)S(1)} %get-tuple-element.41), channel_id=1, source_target_pairs={{0,2},{1,3},{2,0},{3,1},{4,6},{5,7},{6,4},{7,5},{8,10},{9,11},{10,... | collective-permute-start | bytes 393224 | tf_op jit(solution)/shard_map/ppermute | solution.py:219
  52.8 6.8 %collective-permute-start.13 = (f32[8,32,128]{2,1,0:T(8,128)S(1)}, f32[8,32,128]{2,1,0:T(8,128)S(1)}, u32[]{:S(2)}, u32[]{:S(2)}) collective-permute-start(f32[8,32,128]{2,1,0:T(8,128)S(1)} %get-tuple-element.42), channel_id=1, source_target_pairs={{0,3},{1,2},{2,1},{3,0},{4,7},{5,6},{6,5},{7,4},{8,11},{9,10},{10,... | collective-permute-start | bytes 393224 | tf_op jit(solution)/shard_map/ppermute | solution.py:219

commit v3 on v2

--- a/solution.py
+++ b/solution.py
@@ -10,6 +10,7 @@
 epsilon = 1e-06
 unroll = 4
 late_slots = 1
+ahead_count = 2
 
 
 class Dims:
@@ -168,31 +169,44 @@
     lax.fori_loop(0, pl.cdiv(found, unroll), group, 0)
 
 
+def ahead(n):
+    return range(n.rows_axis // 2, min(n.rows_axis // 2 + ahead_count, n.rows_axis))
+
+
+def ahead_kernel(n, kept, core, chip, *outs):
+    for out, o in zip(outs, ahead(n)):
+        out[...] = kept[o] + core[0, o] + chip[o]
+
+
 def spread_kernel(n, *refs):
-    halves = [refs[:3], refs[3:6]]
+    chunks = [refs[:3], refs[3:6]]
     outs = refs[6:]
     for o in range(n.rows_axis):
         at = 0
-        for kept, core, chip in halves:
+        for kept, core, chip in chunks[o in ahead(n) :]:
             rows = kept.shape[1]
             outs[o][pl.ds(at, rows), :] = kept[o] + core[0, o] + chip[o]
             at += rows
 
 
-def gather_kernel(n, lists, *refs):
+def gather_kernel(n, first, lists, *refs):
     parts = refs[: n.rows_axis]
-    outs = refs[n.rows_axis : n.rows_axis + n.grp_axis]
-    total, acc = refs[n.rows_axis + n.grp_axis :]
+    early = dict(zip(ahead(n), refs[n.rows_axis : n.rows_axis + len(ahead(n))]))
+    refs = refs[n.rows_axis + len(ahead(n)) :]
+    outs = refs[: n.grp_axis]
+    total, acc = refs[n.grp_axis :]
     me = lax.axis_index("rows")
     g = lax.axis_index("grp")
     acc[...] = jnp.zeros_like(acc)
     column = jnp.zeros((2 * n.own, n.width), jnp.float32)
     for o in range(n.rows_axis):
         source = jnp.bitwise_xor(me, o)
+        skipped = first if o in early else 0
         for k in range(n.cap):
             i = lists[source, k, me] - me * n.region
-            acc[i] += parts[o][pl.ds(k * n.part, n.part), :]
-        column = column + parts[o][pl.ds(n.cap * n.part, 2 * n.own), :]
+            part, at = (early[o], k) if k < skipped else (parts[o], k - skipped)
+            acc[i] += part[pl.ds(at * n.part, n.part), :]
+        column = column + parts[o][pl.ds((n.cap - skipped) * n.part, 2 * n.own), :]
     total[...] = column
     for d in range(n.grp_axis):
         outs[d][...] = acc[pl.ds(jnp.bitwise_xor(g, d) * n.own, n.own)]
@@ -303,26 +317,41 @@
         name="late_tiles",
     )(lists, pair_count, pairs, sample_rows, matrix, sent)
 
+    first_rows = (first * n.part, n.width)
+    spread_ahead = pl.pallas_call(
+        functools.partial(ahead_kernel, n),
+        out_shape=[jax.ShapeDtypeStruct(first_rows, f32)] * len(ahead(n)),
+        in_specs=[vmem] * 3,
+        out_specs=[vmem] * len(ahead(n)),
+        compiler_params=megabytes((4 * n.rows_axis,) + first_rows),
+        name="ahead",
+    )(*early_sums)
+    came_ahead = []
+    for o, part in zip(ahead(n), spread_ahead):
+        came_ahead.append(swap(part, "rows", n.rows_axis, o))
     halves = early_sums + reduce_scatter(late)[0]
     message = (n.cap * n.part + 2 * n.own, n.width)
-    small = megabytes((4 * n.rows_axis,) + message)
+    shorter = (message[0] - first_rows[0], n.width)
     spread = pl.pallas_call(
         functools.partial(spread_kernel, n),
-        out_shape=[jax.ShapeDtypeStruct(message, f32)] * n.rows_axis,
+        out_shape=[
+            jax.ShapeDtypeStruct(shorter if o in ahead(n) else message, f32) for o in range(n.rows_axis)
+        ],
         in_specs=[vmem] * 6,
         out_specs=[vmem] * n.rows_axis,
-        compiler_params=small,
+        compiler_params=megabytes((4 * n.rows_axis,) + message),
         name="spread",
     )(*halves)
     came = [spread[0]]
     for o in range(1, n.rows_axis):
         came.append(swap(spread[o], "rows", n.rows_axis, o))
+    came += came_ahead
     quarter = (n.own, n.part, n.width)
     *owned, total = pl.pallas_call(
-        functools.partial(gather_kernel, n),
+        functools.partial(gather_kernel, n, first),
         out_shape=[jax.ShapeDtypeStruct(quarter, f32)] * n.grp_axis
         + [jax.ShapeDtypeStruct((2 * n.own, n.width), f32)],
-        in_specs=[smem] + [vmem] * n.rows_axis,
+        in_specs=[smem] + [vmem] * len(came),
         out_specs=[vmem] * (n.grp_axis + 1),
         scratch_shapes=[pltpu.VMEM((n.region, n.part, n.width), f32)],
         compiler_params=megabytes((n.rows_axis,) + message, (2 * n.grp_axis,) + quarter),

time: 60.8 us -> 60 us (0.987)
  waiting for transfers between devices: 27.1 us -> 22.9 us
  starting transfers between devices: 18.5 us -> 22 us
    ppermute x14 -> x16, waiting for transfers between devices: 27.1 us -> 22.9 us  [swap(): return lax.ppermute(x, axis, [(i, i ^ distance) for i in range(size)])]
    ppermute x14 -> x16, starting transfers between devices: 18.5 us -> 22 us  [swap(): return lax.ppermute(x, axis, [(i, i ^ distance) for i in range(size)])]
  transfers between devices with their start and end apart: 14 -> 16, of which waited for: 6 -> 9; matrix products, arithmetic and copies ran while one was open for 0% -> 0% of each run, Pallas kernels for 0% -> 1%
where the time goes in v3:
time: 60 us; the launch traced here: 59.7 us
  waiting for transfers between devices  22.9 us (38%)
  starting transfers between devices  22 us (37%)
  Pallas kernels  14.6 us (24%)
    ppermute x16, waiting for transfers between devices, swap(): return lax.ppermute(x, axis, [(i, i ^ distance) for i in range(size)])  22.9 us
    ppermute x16, starting transfers between devices, swap(): return lax.ppermute(x, axis, [(i, i ^ distance) for i in range(size)])  22 us
    pallas_call x1, Pallas kernels, shards(): pl.pallas_call(functools.partial(early_kernel, n, first), out_shape=stage...  6.68 us
    pallas_call x1, Pallas kernels, shards(): pl.pallas_call(functools.partial(late_kernel, n, first), out_shape=stage_...  5.74 us
  transfers between devices with their start and end apart: 16, of which 9 were waited for; matrix products, arithmetic and copies ran while one was open for 0% of the time, Pallas kernels for 1%

profile of v3, /device:TPU:1, one launch (start us, length us, event | category | flops | bytes accessed | tf_op | source)
XLA Modules:
  0.0 59.7 jit_solution(10969698216305238007)
XLA Ops:
  0.0 6.7 %early_tiles.1 = (f32[2,8,96,128]{3,2,1,0:T(8,128)S(1)}, f32[8,96,128]{2,1,0:T(8,128)S(1)}, f32[8,96,128]{2,1,0:T(8,128)S(1)}) custom-call(s32[8,4,8]{2,1,0:T(4,128)} %bitcast.10, s32[8,8]{1,0:T(8,128)} %counts.3, s32[2,256]{1,0:T(2,128)} %bitcast.13, s32[1,128,256]{2,1,0:T(8,128)} %samples.3, bf16[320,16384]{1,0:T(8,128)(2,1)} %matrix.3), custom_call_target="tpu_custom_call" | custom-call | tf_op jit(solution)/shard_map/early_tiles/pallas_call | solution.py:261
  6.7 0.0 copy-start.2
  6.7 0.1 collective-permute-start
  6.8 2.3 %collective-permute-done.refs_1_.core = f32[2,8,96,128]{3,2,1,0:T(8,128)S(1)} collective-permute-done((f32[2,8,96,128]{3,2,1,0:T(8,128)S(1)}, f32[2,8,96,128]{3,2,1,0:T(8,128)S(1)}, u32[]{:S(2)}, u32[]{:S(2)}) %collective-permute-start) | collective-permute-done | bytes 786464 | tf_op jit(solution)/shard_map/ppermute | solution.py:233
  9.1 5.7 %late_tiles.1 = (f32[2,8,48,128]{3,2,1,0:T(8,128)S(1)}, f32[8,48,128]{2,1,0:T(8,128)S(1)}, f32[8,48,128]{2,1,0:T(8,128)S(1)}) custom-call(s32[8,4,8]{2,1,0:T(4,128)} %bitcast.11, s32[8,8]{1,0:T(8,128)} %counts.3, s32[2,256]{1,0:T(2,128)} %bitcast.14, s32[1,128,256]{2,1,0:T(8,128)S(1)} %copy-done.1, bf16[320,16384]{1,0:T(8,128)(2,1)S(1)} %copy-done, ...), custom_call_target="tpu_custom_call" | custom-call | flops 267386880 | bytes 10485760 | tf_op jit(solution)/shard_map/late_tiles/pallas_call | solution.py:299
  14.9 0.2 collective-permute-start.2
  15.1 2.6 %collective-permute-start.1 = (f32[8,96,128]{2,1,0:T(8,128)S(1)}, f32[8,96,128]{2,1,0:T(8,128)S(1)}, u32[]{:S(2)}, u32[]{:S(2)}) collective-permute-start(f32[8,96,128]{2,1,0:T(8,128)S(1)} %fusion.after), channel_id=1, source_target_pairs={{0,2},{1,3},{2,0},{3,1},{4,6},{5,7},{6,4},{7,5},{8,10},{9,11},{10,... | collective-permute-start | bytes 1179656 | tf_op jit(solution)/shard_map/ppermute | solution.py:233
  17.7 0.0 collective-permute-done.2.refs_4_
  17.7 1.4 %collective-permute-start.3 = (f32[8,48,128]{2,1,0:T(8,128)S(1)}, f32[8,48,128]{2,1,0:T(8,128)S(1)}, u32[]{:S(2)}, u32[]{:S(2)}) collective-permute-start(f32[8,48,128]{2,1,0:T(8,128)S(1)} %fusion.1), channel_id=1, source_target_pairs={{0,2},{1,3},{2,0},{3,1},{4,6},{5,7},{6,4},{7,5},{8,10},{9,11},{10,... | collective-permute-start | bytes 589832 | tf_op jit(solution)/shard_map/ppermute | solution.py:233
  19.1 7.9 %collective-permute-done.1.refs_2_.chip = f32[8,96,128]{2,1,0:T(8,128)S(1)} collective-permute-done((f32[8,96,128]{2,1,0:T(8,128)S(1)}, f32[8,96,128]{2,1,0:T(8,128)S(1)}, u32[]{:S(2)}, u32[]{:S(2)}) %collective-permute-start.1) | collective-permute-done | bytes 393248 | tf_op jit(solution)/shard_map/ppermute | solution.py:233
  27.0 1.7 %collective-permute-start.11 = (f32[96,128]{1,0:T(8,128)S(1)}, f32[96,128]{1,0:T(8,128)S(1)}, u32[]{:S(2)}, u32[]{:S(2)}) collective-permute-start(f32[96,128]{1,0:T(8,128)S(1)} %get-tuple-element.40), channel_id=1, source_target_pairs={{0,16},{4,20},{8,24},{12,28},{16,0},{20,4},{24,8},{28,12},{1,17},{... | collective-permute-start | bytes 147464 | tf_op jit(solution)/shard_map/ppermute | solution.py:233
  28.8 1.0 %collective-permute-start.12 = (f32[96,128]{1,0:T(8,128)S(1)}, f32[96,128]{1,0:T(8,128)S(1)}, u32[]{:S(2)}, u32[]{:S(2)}) collective-permute-start(f32[96,128]{1,0:T(8,128)S(1)} %get-tuple-element.41), channel_id=1, source_target_pairs={{0,20},{4,16},{8,28},{12,24},{16,4},{20,0},{24,12},{28,8},{1,21},{... | collective-permute-start | bytes 147464 | tf_op jit(solution)/shard_map/ppermute | solution.py:233
  29.8 1.5 %collective-permute-done.3.refs_5_ = f32[8,48,128]{2,1,0:T(8,128)S(1)} collective-permute-done((f32[8,48,128]{2,1,0:T(8,128)S(1)}, f32[8,48,128]{2,1,0:T(8,128)S(1)}, u32[]{:S(2)}, u32[]{:S(2)}) %collective-permute-start.3) | collective-permute-done | bytes 196640 | tf_op jit(solution)/shard_map/ppermute | solution.py:233
  31.2 0.1 spread.1
  31.3 1.7 %collective-permute-start.7 = (f32[48,128]{1,0:T(8,128)S(1)}, f32[48,128]{1,0:T(8,128)S(1)}, u32[]{:S(2)}, u32[]{:S(2)}) collective-permute-start(f32[48,128]{1,0:T(8,128)S(1)} %get-tuple-element.36), channel_id=1, source_target_pairs={{0,16},{4,20},{8,24},{12,28},{16,0},{20,4},{24,8},{28,12},{1,17},{... | collective-permute-start | bytes 73736 | tf_op jit(solution)/shard_map/ppermute | solution.py:233
  33.0 1.0 %collective-permute-start.8 = (f32[48,128]{1,0:T(8,128)S(1)}, f32[48,128]{1,0:T(8,128)S(1)}, u32[]{:S(2)}, u32[]{:S(2)}) collective-permute-start(f32[48,128]{1,0:T(8,128)S(1)} %get-tuple-element.37), channel_id=1, source_target_pairs={{0,20},{4,16},{8,28},{12,24},{16,4},{20,0},{24,12},{28,8},{1,21},{... | collective-permute-start | bytes 73736 | tf_op jit(solution)/shard_map/ppermute | solution.py:233
  34.0 3.3 %collective-permute-start.10 = (f32[144,128]{1,0:T(8,128)S(1)}, f32[144,128]{1,0:T(8,128)S(1)}, u32[]{:S(2)}, u32[]{:S(2)}) collective-permute-start(f32[144,128]{1,0:T(8,128)S(1)} %get-tuple-element.39), channel_id=1, source_target_pairs={{0,28},{4,24},{8,20},{12,16},{16,12},{20,8},{24,4},{28,0},{1,29},{... | collective-permute-start | bytes 221192 | tf_op jit(solution)/shard_map/ppermute | solution.py:233
  37.3 1.8 %collective-permute-start.4 = (f32[144,128]{1,0:T(8,128)S(1)}, f32[144,128]{1,0:T(8,128)S(1)}, u32[]{:S(2)}, u32[]{:S(2)}) collective-permute-start(f32[144,128]{1,0:T(8,128)S(1)} %get-tuple-element.33), channel_id=1, source_target_pairs={{0,4},{4,0},{8,12},{12,8},{16,20},{20,16},{24,28},{28,24},{1,5},{5... | collective-permute-start | bytes 221192 | tf_op jit(solution)/shard_map/ppermute | solution.py:233
  39.1 1.2 %collective-permute-start.6 = (f32[144,128]{1,0:T(8,128)S(1)}, f32[144,128]{1,0:T(8,128)S(1)}, u32[]{:S(2)}, u32[]{:S(2)}) collective-permute-start(f32[144,128]{1,0:T(8,128)S(1)} %get-tuple-element.35), channel_id=1, source_target_pairs={{0,12},{4,8},{8,4},{12,0},{16,28},{20,24},{24,20},{28,16},{1,13},{... | collective-permute-start | bytes 221192 | tf_op jit(solution)/shard_map/ppermute | solution.py:233
  40.4 0.2 collective-permute-start.9
  40.6 0.5 collective-permute-done.4.refs_1_
  41.1 1.8 %collective-permute-done.5.refs_2_ = f32[144,128]{1,0:T(8,128)S(1)} collective-permute-done((f32[144,128]{1,0:T(8,128)S(1)}, f32[144,128]{1,0:T(8,128)S(1)}, u32[]{:S(2)}, u32[]{:S(2)}) %collective-permute-start.5) | collective-permute-done | bytes 73760 | tf_op jit(solution)/shard_map/ppermute | solution.py:233
  42.9 0.8 %collective-permute-done.6.refs_3_ = f32[144,128]{1,0:T(8,128)S(1)} collective-permute-done((f32[144,128]{1,0:T(8,128)S(1)}, f32[144,128]{1,0:T(8,128)S(1)}, u32[]{:S(2)}, u32[]{:S(2)}) %collective-permute-start.6) | collective-permute-done | bytes 73760 | tf_op jit(solution)/shard_map/ppermute | solution.py:233
  43.8 2.0 %collective-permute-done.9.refs_6_ = f32[144,128]{1,0:T(8,128)S(1)} collective-permute-done((f32[144,128]{1,0:T(8,128)S(1)}, f32[144,128]{1,0:T(8,128)S(1)}, u32[]{:S(2)}, u32[]{:S(2)}) %collective-permute-start.9) | collective-permute-done | bytes 73760 | tf_op jit(solution)/shard_map/ppermute | solution.py:233
  45.8 1.0 %gather.1 = (f32[8,32,128]{2,1,0:T(8,128)S(1)}, f32[8,32,128]{2,1,0:T(8,128)S(1)}, f32[8,32,128]{2,1,0:T(8,128)S(1)}, f32[8,32,128]{2,1,0:T(8,128)S(1)}, f32[16,128]{1,0:T(8,128)S(1)}) custom-call(s32[8,4,8]{2,1,0:T(4,128)S(1)} %bitcast.12, f32[144,128]{1,0:T(8,128)S(1)} %get-tuple-element.32.refs_0_, f32[144,128]{1,0:T(8,128)S(1)} %collective-permute-done.4.refs_1_, ...), custom_call_target="tpu_custom_call" | custom-call | tf_op jit(solution)/shard_map/gather/pallas_call | solution.py:350
  46.8 4.0 %collective-permute-start.13 = (f32[8,32,128]{2,1,0:T(8,128)S(1)}, f32[8,32,128]{2,1,0:T(8,128)S(1)}, u32[]{:S(2)}, u32[]{:S(2)}) collective-permute-start(f32[8,32,128]{2,1,0:T(8,128)S(1)} %get-tuple-element.44), channel_id=1, source_target_pairs={{0,1},{1,0},{2,3},{3,2},{4,5},{5,4},{6,7},{7,6},{8,9},{9,8},{10,11... | collective-permute-start | bytes 393224 | tf_op jit(solution)/shard_map/ppermute | solution.py:233
  50.8 1.2 %collective-permute-start.14 = (f32[8,32,128]{2,1,0:T(8,128)S(1)}, f32[8,32,128]{2,1,0:T(8,128)S(1)}, u32[]{:S(2)}, u32[]{:S(2)}) collective-permute-start(f32[8,32,128]{2,1,0:T(8,128)S(1)} %get-tuple-element.45), channel_id=1, source_target_pairs={{0,2},{1,3},{2,0},{3,1},{4,6},{5,7},{6,4},{7,5},{8,10},{9,11},{10,... | collective-permute-start | bytes 393224 | tf_op jit(solution)/shard_map/ppermute | solution.py:233
  52.1 0.5 collective-permute-start.15
  52.5 0.2 factor.1
  52.8 3.0 %collective-permute-done.14.refs_2_ = f32[8,32,128]{2,1,0:T(8,128)S(1)} collective-permute-done((f32[8,32,128]{2,1,0:T(8,128)S(1)}, f32[8,32,128]{2,1,0:T(8,128)S(1)}, u32[]{:S(2)}, u32[]{:S(2)}) %collective-permute-start.14) | collective-permute-done | bytes 131104 | tf_op jit(solution)/shard_map/ppermute | solution.py:233
  55.8 3.1 %collective-permute-done.15.refs_3_ = f32[8,32,128]{2,1,0:T(8,128)S(1)} collective-permute-done((f32[8,32,128]{2,1,0:T(8,128)S(1)}, f32[8,32,128]{2,1,0:T(8,128)S(1)}, u32[]{:S(2)}, u32[]{:S(2)}) %collective-permute-start.15) | collective-permute-done | bytes 131104 | tf_op jit(solution)/shard_map/ppermute | solution.py:233
  58.9 0.8 %scale.1 = f32[8,128,128]{2,1,0:T(8,128)} custom-call(f32[8,128,128]{2,1,0:T(8,128)S(1)} %factor.1, f32[8,32,128]{2,1,0:T(8,128)S(1)} %get-tuple-element.43.refs_0_, f32[8,32,128]{2,1,0:T(8,128)S(1)} %collective-permute-done.13.refs_1_, f32[8,32,128]{2,1,0:T(8,128)S(1)} %collective-permute-done.14.refs_2_, f32[8,32,128]{2,1,0:T(8,128)S(1)} %collective-permute-done.15.refs_3_), custom_call_target="tpu_custom_call" | custom-call | tf_op jit(solution)/shard_map/scale/pallas_call | solution.py:372
  (15 shorter events, 0.1 us)
Async XLA Ops:
  0.0 9.1 %copy-start = (bf16[320,16384]{1,0:T(8,128)(2,1)S(1)}, bf16[320,16384]{1,0:T(8,128)(2,1)}, u32[]{:S(2)}) copy-start(bf16[320,16384]{1,0:T(8,128)(2,1)} %matrix.3) | copy-start | bytes 31457284
  0.0 9.1 %copy-start.1 = (s32[1,128,256]{2,1,0:T(8,128)S(1)}, s32[1,128,256]{2,1,0:T(8,128)}, u32[]{:S(2)}) copy-start(s32[1,128,256]{2,1,0:T(8,128)} %samples.3) | copy-start | bytes 393220
  6.7 39.1 %copy-start.2 = (s32[8,8,4]{1,2,0:T(4,128)S(1)}, s32[8,8,4]{1,2,0:T(4,128)}, u32[]{:S(2)}) copy-start(s32[8,8,4]{1,2,0:T(4,128)} %param.7) | copy-start | bytes 3076
  6.7 2.4 %collective-permute-start = (f32[2,8,96,128]{3,2,1,0:T(8,128)S(1)}, f32[2,8,96,128]{3,2,1,0:T(8,128)S(1)}, u32[]{:S(2)}, u32[]{:S(2)}) collective-permute-start(f32[2,8,96,128]{3,2,1,0:T(8,128)S(1)} %get-tuple-element.27), channel_id=1, source_target_pairs={{0,1},{1,0},{2,3},{3,2},{4,5},{5,4},{6,7},{7,6},{8,9},{9,8},{10,11... | collective-permute-start | bytes 2359304 | tf_op jit(solution)/shard_map/ppermute | solution.py:233
  14.9 2.8 %collective-permute-start.2 = (f32[2,8,48,128]{3,2,1,0:T(8,128)S(1)}, f32[2,8,48,128]{3,2,1,0:T(8,128)S(1)}, u32[]{:S(2)}, u32[]{:S(2)}) collective-permute-start(f32[2,8,48,128]{3,2,1,0:T(8,128)S(1)} %get-tuple-element.30), channel_id=1, source_target_pairs={{0,1},{1,0},{2,3},{3,2},{4,5},{5,4},{6,7},{7,6},{8,9},{9,8},{10,11... | collective-permute-start | bytes 1179656 | tf_op jit(solution)/shard_map/ppermute | solution.py:233
  15.1 11.9 %collective-permute-start.1 = (f32[8,96,128]{2,1,0:T(8,128)S(1)}, f32[8,96,128]{2,1,0:T(8,128)S(1)}, u32[]{:S(2)}, u32[]{:S(2)}) collective-permute-start(f32[8,96,128]{2,1,0:T(8,128)S(1)} %fusion.after), channel_id=1, source_target_pairs={{0,2},{1,3},{2,0},{3,1},{4,6},{5,7},{6,4},{7,5},{8,10},{9,11},{10,... | collective-permute-start | bytes 1179656 | tf_op jit(solution)/shard_map/ppermute | solution.py:233
  17.7 13.5 %collective-permute-start.3 = (f32[8,48,128]{2,1,0:T(8,128)S(1)}, f32[8,48,128]{2,1,0:T(8,128)S(1)}, u32[]{:S(2)}, u32[]{:S(2)}) collective-permute-start(f32[8,48,128]{2,1,0:T(8,128)S(1)} %fusion.1), channel_id=1, source_target_pairs={{0,2},{1,3},{2,0},{3,1},{4,6},{5,7},{6,4},{7,5},{8,10},{9,11},{10,... | collective-permute-start | bytes 589832 | tf_op jit(solution)/shard_map/ppermute | solution.py:233
  27.0 10.3 %collective-permute-start.11 = (f32[96,128]{1,0:T(8,128)S(1)}, f32[96,128]{1,0:T(8,128)S(1)}, u32[]{:S(2)}, u32[]{:S(2)}) collective-permute-start(f32[96,128]{1,0:T(8,128)S(1)} %get-tuple-element.40), channel_id=1, source_target_pairs={{0,16},{4,20},{8,24},{12,28},{16,0},{20,4},{24,8},{28,12},{1,17},{... | collective-permute-start | bytes 147464 | tf_op jit(solution)/shard_map/ppermute | solution.py:233
  28.8 10.4 %collective-permute-start.12 = (f32[96,128]{1,0:T(8,128)S(1)}, f32[96,128]{1,0:T(8,128)S(1)}, u32[]{:S(2)}, u32[]{:S(2)}) collective-permute-start(f32[96,128]{1,0:T(8,128)S(1)} %get-tuple-element.41), channel_id=1, source_target_pairs={{0,20},{4,16},{8,28},{12,24},{16,4},{20,0},{24,12},{28,8},{1,21},{... | collective-permute-start | bytes 147464 | tf_op jit(solution)/shard_map/ppermute | solution.py:233
  31.3 7.8 %collective-permute-start.7 = (f32[48,128]{1,0:T(8,128)S(1)}, f32[48,128]{1,0:T(8,128)S(1)}, u32[]{:S(2)}, u32[]{:S(2)}) collective-permute-start(f32[48,128]{1,0:T(8,128)S(1)} %get-tuple-element.36), channel_id=1, source_target_pairs={{0,16},{4,20},{8,24},{12,28},{16,0},{20,4},{24,8},{28,12},{1,17},{... | collective-permute-start | bytes 73736 | tf_op jit(solution)/shard_map/ppermute | solution.py:233
  33.0 7.3 %collective-permute-start.8 = (f32[48,128]{1,0:T(8,128)S(1)}, f32[48,128]{1,0:T(8,128)S(1)}, u32[]{:S(2)}, u32[]{:S(2)}) collective-permute-start(f32[48,128]{1,0:T(8,128)S(1)} %get-tuple-element.37), channel_id=1, source_target_pairs={{0,20},{4,16},{8,28},{12,24},{16,4},{20,0},{24,12},{28,8},{1,21},{... | collective-permute-start | bytes 73736 | tf_op jit(solution)/shard_map/ppermute | solution.py:233
  34.0 6.6 %collective-permute-start.10 = (f32[144,128]{1,0:T(8,128)S(1)}, f32[144,128]{1,0:T(8,128)S(1)}, u32[]{:S(2)}, u32[]{:S(2)}) collective-permute-start(f32[144,128]{1,0:T(8,128)S(1)} %get-tuple-element.39), channel_id=1, source_target_pairs={{0,28},{4,24},{8,20},{12,16},{16,12},{20,8},{24,4},{28,0},{1,29},{... | collective-permute-start | bytes 221192 | tf_op jit(solution)/shard_map/ppermute | solution.py:233
  37.3 3.8 %collective-permute-start.4 = (f32[144,128]{1,0:T(8,128)S(1)}, f32[144,128]{1,0:T(8,128)S(1)}, u32[]{:S(2)}, u32[]{:S(2)}) collective-permute-start(f32[144,128]{1,0:T(8,128)S(1)} %get-tuple-element.33), channel_id=1, source_target_pairs={{0,4},{4,0},{8,12},{12,8},{16,20},{20,16},{24,28},{28,24},{1,5},{5... | collective-permute-start | bytes 221192 | tf_op jit(solution)/shard_map/ppermute | solution.py:233
  39.1 3.8 %collective-permute-start.5 = (f32[144,128]{1,0:T(8,128)S(1)}, f32[144,128]{1,0:T(8,128)S(1)}, u32[]{:S(2)}, u32[]{:S(2)}) collective-permute-start(f32[144,128]{1,0:T(8,128)S(1)} %get-tuple-element.34), channel_id=1, source_target_pairs={{0,8},{4,12},{8,0},{12,4},{16,24},{20,28},{24,16},{28,20},{1,9},{5... | collective-permute-start | bytes 221192 | tf_op jit(solution)/shard_map/ppermute | solution.py:233
  39.1 4.6 %collective-permute-start.6 = (f32[144,128]{1,0:T(8,128)S(1)}, f32[144,128]{1,0:T(8,128)S(1)}, u32[]{:S(2)}, u32[]{:S(2)}) collective-permute-start(f32[144,128]{1,0:T(8,128)S(1)} %get-tuple-element.35), channel_id=1, source_target_pairs={{0,12},{4,8},{8,4},{12,0},{16,28},{20,24},{24,20},{28,16},{1,13},{... | collective-permute-start | bytes 221192 | tf_op jit(solution)/shard_map/ppermute | solution.py:233
  40.4 5.4 %collective-permute-start.9 = (f32[144,128]{1,0:T(8,128)S(1)}, f32[144,128]{1,0:T(8,128)S(1)}, u32[]{:S(2)}, u32[]{:S(2)}) collective-permute-start(f32[144,128]{1,0:T(8,128)S(1)} %get-tuple-element.38), channel_id=1, source_target_pairs={{0,24},{4,28},{8,16},{12,20},{16,8},{20,12},{24,0},{28,4},{1,25},{... | collective-permute-start | bytes 221192 | tf_op jit(solution)/shard_map/ppermute | solution.py:233
  46.8 5.9 %collective-permute-start.13 = (f32[8,32,128]{2,1,0:T(8,128)S(1)}, f32[8,32,128]{2,1,0:T(8,128)S(1)}, u32[]{:S(2)}, u32[]{:S(2)}) collective-permute-start(f32[8,32,128]{2,1,0:T(8,128)S(1)} %get-tuple-element.44), channel_id=1, source_target_pairs={{0,1},{1,0},{2,3},{3,2},{4,5},{5,4},{6,7},{7,6},{8,9},{9,8},{10,11... | collective-permute-start | bytes 393224 | tf_op jit(solution)/shard_map/ppermute | solution.py:233
  50.8 5.0 %collective-permute-start.14 = (f32[8,32,128]{2,1,0:T(8,128)S(1)}, f32[8,32,128]{2,1,0:T(8,128)S(1)}, u32[]{:S(2)}, u32[]{:S(2)}) collective-permute-start(f32[8,32,128]{2,1,0:T(8,128)S(1)} %get-tuple-element.45), channel_id=1, source_target_pairs={{0,2},{1,3},{2,0},{3,1},{4,6},{5,7},{6,4},{7,5},{8,10},{9,11},{10,... | collective-permute-start | bytes 393224 | tf_op jit(solution)/shard_map/ppermute | solution.py:233
  52.1 6.8 %collective-permute-start.15 = (f32[8,32,128]{2,1,0:T(8,128)S(1)}, f32[8,32,128]{2,1,0:T(8,128)S(1)}, u32[]{:S(2)}, u32[]{:S(2)}) collective-permute-start(f32[8,32,128]{2,1,0:T(8,128)S(1)} %get-tuple-element.46), channel_id=1, source_target_pairs={{0,3},{1,2},{2,1},{3,0},{4,7},{5,6},{6,5},{7,4},{8,11},{9,10},{10,... | collective-permute-start | bytes 393224 | tf_op jit(solution)/shard_map/ppermute | solution.py:233
